TPU v7x, 256 devices: a whole 4x4x8 slice. The times are simulated.
256 devices in a mesh: graph: 16 (over z, y_lo), row: 16 (over y_hi, x, core).
Axes of the slice: x: 4, y: 4 (y_hi: 2, y_lo: 2; y = y_hi * 2 + y_lo), z: 8, core: 2. Of those that a mesh axis runs over, the one named last changes fastest.
Arguments:
- tiles: bfloat16 [16384, 256, 256], P(('graph', 'row')), parts along dimension 0, may hold values from -0.25 to 0.25
- tile_rows: int32 [16384], P(('graph', 'row')), parts along dimension 0, may hold values from 0 to 15
- tile_cols: int32 [16384], P(('graph', 'row')), parts along dimension 0, may hold values from 0 to 255, as said below
- tile_count: int32 [256], P(('graph', 'row')), parts along dimension 0, may hold values from 8 to 64, as said below
- seeds: float32 [32, 1048576], P(None, ('graph', 'row')), parts along dimension 1, may hold values from -6 to 6
- decay: float32 [32], replicated, may hold values from 0.8 to 1
Outputs:
- scores: float32 [32, 1048576], P(None, ('graph', 'row')), parts along dimension 1
There are 16 independent parts, one for each index of `graph`. A program takes and returns all parts, laid end to end along the dimension named above; an argument that names none is the same for every part. Nothing has to cross between parts.
Inputs may be any that keep to these rules, and one draw needn't show every extreme that they name: `tile_cols`: among the slots of one row panel, the tile columns that fall in the 16 tile rows of any one panel take at most 4 distinct values; in every draw the live slots of some panel take exactly 4 distinct tile columns of some one panel. Only the first tile_count slots of a panel are live; in every draw one panel has all 64 slots live.
All inputs are finite; a program needn't handle non-finite values.
Results may differ from a plain program's by a relative error of at most 0.0027.
Values may be sent and summed in bfloat16 or wider, within the bound.
No kernel may reach another device: no remote copies, remote signals or barrier semaphores. Data moves between devices by JAX's collectives and lax.ppermute only.
A program may use at most 64 MiB of HBM per device.

v0:
```python
import jax
import jax.numpy as jnp
from jax import lax
from jax.sharding import PartitionSpec as P

TILE = 256
NEED = 4
ITERS = 3


def sent_to_all(x, axis):
    copies = jnp.broadcast_to(x, (lax.axis_size(axis), *x.shape))
    return lax.all_to_all(copies, axis, split_axis=0, concat_axis=0, tiled=True)


def of_everyone(x, axis):
    everything = sent_to_all(x, axis)
    return jnp.sum(everything, axis=0)


def per_device(tiles, tile_rows, tile_cols, tile_count, seeds, decay):
    count_of_slots = tiles.shape[0]
    seed_count = seeds.shape[0]
    blk_local = seeds.shape[1] // TILE
    panel_total = lax.axis_size("row")
    active_flag = jnp.arange(count_of_slots, dtype=jnp.int32) < tile_count[0]
    matches = tile_rows[:, None] == jnp.arange(blk_local, dtype=jnp.int32)[None, :]
    indicator_matrix = (matches & active_flag[:, None]).astype(jnp.float32)
    owner_of = tile_cols // blk_local
    local_of = tile_cols % blk_local
    owner_hit = owner_of[:, None] == jnp.arange(panel_total, dtype=jnp.int32)[None, :]
    local_match = local_of[:, None] == jnp.arange(blk_local, dtype=jnp.int32)[None, :]
    live_owner = (owner_hit & active_flag[:, None]).astype(jnp.int32)
    present = jnp.einsum("tq,tb->qb", live_owner, local_match.astype(jnp.int32)) > 0
    ranking = jnp.cumsum(present.astype(jnp.int32), axis=1) - 1
    rank_hit = present[:, :, None] & (
        ranking[:, :, None] == jnp.arange(NEED, dtype=jnp.int32)[None, None, :]
    )
    block_ids = jnp.arange(blk_local, dtype=jnp.int32)[None, :, None]
    wanted = jnp.sum(jnp.where(rank_hit, block_ids, 0), axis=1)
    asked = lax.all_to_all(wanted, "row", split_axis=0, concat_axis=0, tiled=True)
    asked_flat = asked.reshape(panel_total * NEED)
    slot_rank = ranking[owner_of, local_of]
    slot_place = jnp.clip(owner_of * NEED + slot_rank, 0, panel_total * NEED - 1)
    iterate = seeds
    for step in range(ITERS):
        rounded = iterate.astype(jnp.bfloat16)
        own_blocks = rounded.reshape(seed_count, blk_local, TILE)
        outgoing = jnp.take(own_blocks, asked_flat, axis=1).reshape(
            seed_count, panel_total, NEED * TILE
        )
        arrived = lax.all_to_all(outgoing, "row", split_axis=1, concat_axis=1, tiled=True)
        arrived = arrived.reshape(seed_count, panel_total * NEED, TILE)
        picked = jnp.take(arrived, slot_place, axis=1)
        block_products = jnp.einsum(
            "trc,stc->str", tiles, picked, preferred_element_type=jnp.float32
        )
        reduced_sum = jnp.einsum(
            "mv,emy->evy", indicator_matrix, block_products, precision=lax.Precision.HIGHEST
        )
        reduced_sum = reduced_sum.reshape(seed_count, blk_local * TILE)
        iterate = decay[:, None] * reduced_sum + seeds
    squares = of_everyone(jnp.sum(iterate * iterate, axis=1), "row")
    total_nodes = panel_total * iterate.shape[1]
    norm_value = jnp.sqrt(squares / total_nodes + 1e-06)
    return iterate / norm_value[:, None]


def solution(mesh):
    in_specs = (
        P(("graph", "row"), None, None),
        P(("graph", "row")),
        P(("graph", "row")),
        P(("graph", "row")),
        P(None, ("graph", "row")),
        P(),
    )
    out_specs = P(None, ("graph", "row"))
    return jax.shard_map(
        per_device, mesh=mesh, in_specs=in_specs, out_specs=out_specs, check_vma=False
    )
```

profile of v0, /device:TPU:1, one launch (start us, length us, event | category | flops | bytes accessed | tf_op | source)
XLA Modules:
  0.0 138.7 jit_solution(12599641336655567563)
XLA Ops:
  0.7 0.7 fusion.37
  1.9 0.7 copy.60
  2.6 8.4 %all-to-all-start = ((s32[16,1,4]{2,1,0:T(1,128)}), s32[16,1,4]{2,1,0:T(1,128)S(1)}, u32[]{:S(2)}, u32[]{:S(2)}) async-start(s32[16,1,4]{2,1,0:T(1,128)} %copy.60), calls=%async_computation | async-start | bytes 16384 | tf_op jit(solution)/shard_map/all_to_all | solution.py:41
  11.0 1.1 convert_element_type.15
  12.1 5.8 %all-to-all-done = s32[16,1,4]{2,1,0:T(1,128)S(1)} async-done(((s32[16,1,4]{2,1,0:T(1,128)}), s32[16,1,4]{2,1,0:T(1,128)S(1)}, u32[]{:S(2)}, u32[]{:S(2)}) %all-to-all-start) | async-done | bytes 288 | tf_op jit(solution)/shard_map/all_to_all | solution.py:41
  17.9 0.5 broadcast.175
  18.4 0.7 reduce.4
  19.2 0.6 gather_fusion.1
  20.0 0.6 copy.62
  20.6 0.7 reshape.75
  21.3 1.6 %copy.63 = bf16[32,16,1024]{2,0,1:T(8,128)(2,1)} copy(bf16[32,16,1024]{2,1,0:T(8,128)(2,1)S(1)} %reshape.75) | data formatting | bytes 2097152 | tf_op jit(solution)/shard_map/reshape | solution.py:49
  22.9 4.1 %all-to-all-start.1 = ((bf16[32,16,1024]{2,0,1:T(8,128)(2,1)}), bf16[32,16,1024]{2,0,1:T(8,128)(2,1)S(1)}, u32[]{:S(2)}, u32[]{:S(2)}) async-start(bf16[32,16,1024]{2,0,1:T(8,128)(2,1)} %copy.63), calls=%async_computation.1 | async-start | bytes 2097152 | tf_op jit(solution)/shard_map/all_to_all | solution.py:52
  27.0 0.8 gather_fusion
  27.8 16.5 %all-to-all-done.1 = bf16[32,16,1024]{2,0,1:T(8,128)(2,1)S(1)} async-done(((bf16[32,16,1024]{2,0,1:T(8,128)(2,1)}), bf16[32,16,1024]{2,0,1:T(8,128)(2,1)S(1)}, u32[]{:S(2)}, u32[]{:S(2)}) %all-to-all-start.1) | async-done | bytes 1048608 | tf_op jit(solution)/shard_map/all_to_all | solution.py:52
  44.4 0.6 copy.64
  44.9 0.7 reshape.76
  45.6 0.6 copy.65
  46.2 0.6 gather_fusion.2
  46.8 5.9 %convolution_bitcast_fusion.2 = f32[32,64,256]{2,0,1:T(8,128)S(1)} fusion(bf16[64,256,256]{2,1,0:T(8,128)(2,1)} %param.10, bf16[64,32,256]{2,1,0:T(8,128)(2,1)S(1)} %gather_fusion.2, pred[64]{0:T(512)(128)(4,1)S(1)} %get-tuple-element.6), kind=kOutput, calls=%fused_computation.15 | convolution fusion | flops 268959744 | bytes 11534400 | tf_op jit(solution)/shard_map/trc,stc->str/dot_general | solution.py:55
  52.8 2.0 %fusion.4 = f32[32,256,16]{1,2,0:T(8,128)S(1)} fusion(f32[32,64,256]{2,0,1:T(8,128)S(1)} %convolution_bitcast_fusion.2, s32[64]{0:T(128)S(1)} %copy-done.2, pred[64]{0:T(512)(128)(4,1)S(1)} %iota_compare_fusion.5), kind=kOutput, calls=%fused_computation.11 | convolution fusion | flops 100665344 | bytes 2621760 | tf_op jit(solution)/shard_map/mv,emy->evy/dot_general | solution.py:58
  54.8 0.3 copy.83
  55.3 0.6 gather_fusion.3
  56.1 0.6 copy.68
  56.6 0.7 reshape.79
  57.3 0.6 copy.69
  57.9 19.9 %all_to_all.30 = bf16[32,16,1024]{2,0,1:T(8,128)(2,1)S(1)} all-to-all(bf16[32,16,1024]{2,0,1:T(8,128)(2,1)S(1)} %copy.69), channel_id=1, replica_groups=mesh['graph'=16,'row'=16] {'row'}, dimensions={1} | all-to-all | bytes 2097152 | tf_op jit(solution)/shard_map/all_to_all | solution.py:52
  77.8 0.6 copy.70
  78.4 1.5 %reshape.80 = bf16[32,64,256]{2,1,0:T(8,128)(2,1)} reshape(bf16[32,16,1024]{2,1,0:T(8,128)(2,1)S(1)} %copy.70) | data formatting | bytes 2097152 | tf_op jit(solution)/shard_map/reshape | solution.py:53
  79.9 1.8 %copy.71 = bf16[32,64,256]{2,0,1:T(8,128)(2,1)S(1)} copy(bf16[32,64,256]{2,1,0:T(8,128)(2,1)} %reshape.80) | data formatting | bytes 2097152 | tf_op jit(solution)/shard_map/reshape | solution.py:53
  81.7 0.6 gather_fusion.4
  82.3 5.9 %convolution_bitcast_fusion.1 = f32[32,64,256]{2,0,1:T(8,128)S(1)} fusion(bf16[64,256,256]{2,1,0:T(8,128)(2,1)} %param.10, bf16[64,32,256]{2,1,0:T(8,128)(2,1)S(1)} %gather_fusion.4, pred[64]{0:T(512)(128)(4,1)S(1)} %get-tuple-element.6), kind=kOutput, calls=%fused_computation.14 | convolution fusion | flops 268959744 | bytes 11534400 | tf_op jit(solution)/shard_map/trc,stc->str/dot_general | solution.py:55
  88.2 2.0 %fusion.2 = f32[32,256,16]{1,2,0:T(8,128)S(1)} fusion(f32[32,64,256]{2,0,1:T(8,128)S(1)} %convolution_bitcast_fusion.1, s32[64]{0:T(128)S(1)} %copy-done.2, pred[64]{0:T(512)(128)(4,1)S(1)} %iota_compare_fusion.5), kind=kOutput, calls=%fused_computation.9 | convolution fusion | flops 100665344 | bytes 2621760 | tf_op jit(solution)/shard_map/mv,emy->evy/dot_general | solution.py:58
  90.2 0.3 copy.84
  90.7 0.6 gather_fusion.5
  91.5 0.6 copy.74
  92.1 0.7 reshape.83
  92.7 0.6 copy.75
  93.3 20.6 %all_to_all.31 = bf16[32,16,1024]{2,0,1:T(8,128)(2,1)S(1)} all-to-all(bf16[32,16,1024]{2,0,1:T(8,128)(2,1)S(1)} %copy.75), channel_id=1, replica_groups=mesh['graph'=16,'row'=16] {'row'}, dimensions={1} | all-to-all | bytes 2097152 | tf_op jit(solution)/shard_map/all_to_all | solution.py:52
  113.9 0.6 copy.76
  114.5 1.5 %reshape.84 = bf16[32,64,256]{2,1,0:T(8,128)(2,1)} reshape(bf16[32,16,1024]{2,1,0:T(8,128)(2,1)S(1)} %copy.76) | data formatting | bytes 2097152 | tf_op jit(solution)/shard_map/reshape | solution.py:53
  116.0 1.8 %copy.77 = bf16[32,64,256]{2,0,1:T(8,128)(2,1)S(1)} copy(bf16[32,64,256]{2,1,0:T(8,128)(2,1)} %reshape.84) | data formatting | bytes 2097152 | tf_op jit(solution)/shard_map/reshape | solution.py:53
  117.8 0.6 gather_fusion.6
  118.4 5.9 %convolution_bitcast_fusion = f32[32,64,256]{2,0,1:T(8,128)S(1)} fusion(bf16[64,256,256]{2,1,0:T(8,128)(2,1)} %param.10, bf16[64,32,256]{2,1,0:T(8,128)(2,1)S(1)} %gather_fusion.6, pred[64]{0:T(512)(128)(4,1)S(1)} %get-tuple-element.6), kind=kOutput, calls=%fused_computation.13 | convolution fusion | flops 268959744 | bytes 11534400 | tf_op jit(solution)/shard_map/trc,stc->str/dot_general | solution.py:55
  124.3 2.0 %fusion = f32[32,256,16]{1,2,0:T(8,128)S(1)} fusion(f32[32,64,256]{2,0,1:T(8,128)S(1)} %convolution_bitcast_fusion, s32[64]{0:T(128)S(1)} %copy-done.2, pred[64]{0:T(512)(128)(4,1)S(1)} %iota_compare_fusion.5), kind=kOutput, calls=%fused_computation.7 | convolution fusion | flops 100665344 | bytes 2621760 | tf_op jit(solution)/shard_map/mv,emy->evy/dot_general | solution.py:58
  126.3 0.3 copy.85
  126.6 0.3 multiply_reduce_fusion
  126.9 10.9 %all_to_all.32 = f32[16,1,32]{2,1,0:T(1,128)S(1)} all-to-all(f32[16,1,32]{2,1,0:T(1,128)S(1)} %broadcast_in_dim.59), channel_id=1, replica_groups=mesh['graph'=16,'row'=16] {'row'}, dimensions={0} | all-to-all | bytes 4096 | tf_op jit(solution)/shard_map/all_to_all | solution.py:13
  137.8 0.9 broadcast_divide_fusion
  (28 shorter events, 1.5 us)
Async XLA Ops:
  2.6 15.4 %all-to-all-start = ((s32[16,1,4]{2,1,0:T(1,128)}), s32[16,1,4]{2,1,0:T(1,128)S(1)}, u32[]{:S(2)}, u32[]{:S(2)}) async-start(s32[16,1,4]{2,1,0:T(1,128)} %copy.60), calls=%async_computation | async-start | bytes 16384 | tf_op jit(solution)/shard_map/all_to_all | solution.py:41
  22.9 21.5 %all-to-all-start.1 = ((bf16[32,16,1024]{2,0,1:T(8,128)(2,1)}), bf16[32,16,1024]{2,0,1:T(8,128)(2,1)S(1)}, u32[]{:S(2)}, u32[]{:S(2)}) async-start(bf16[32,16,1024]{2,0,1:T(8,128)(2,1)} %copy.63), calls=%async_computation.1 | async-start | bytes 2097152 | tf_op jit(solution)/shard_map/all_to_all | solution.py:52
  46.8 5.9 %copy-start.2 = (s32[64]{0:T(128)S(1)}, s32[64]{0:T(128)}, u32[]{:S(2)}) copy-start(s32[64]{0:T(128)} %param.11) | copy-start | bytes 772
  52.8 2.3 %copy-start = (f32[32,4096]{1,0:T(8,128)S(1)}, f32[32,4096]{1,0:T(8,128)}, u32[]{:S(2)}) copy-start(f32[32,4096]{1,0:T(8,128)} %param.14) | copy-start | bytes 1572868
  52.8 2.3 %copy-start.1 = (f32[32]{0:T(128)S(1)}, f32[32]{0:T(128)}, u32[]{:S(2)}) copy-start(f32[32]{0:T(128)} %param.15) | copy-start | bytes 388
where the time goes:
time: 139 us
  blocking collectives  51.4 us (37%)
  matrix products  23.8 us (17%)
  local copies, waits for them, and re-layouts  22.8 us (16%)
  waiting for transfers between devices  22.4 us (16%)
  starting transfers between devices  12.5 us (9%)
  other arithmetic  4.73 us (3%)
    all_to_all x2, blocking collectives, per_device(): lax.all_to_all(outgoing, 'row', split_axis=1, concat_axis=1, tiled=True)  40.5 us
    dot_general x3, matrix products, per_device(): jnp.einsum('trc,stc->str', tiles, picked, preferred_element_type=jnp.floa...  17.7 us
    all_to_all x1, waiting for transfers between devices, per_device(): lax.all_to_all(outgoing, 'row', split_axis=1, concat_axis=1, tiled=True)  16.5 us
    all_to_all x1, blocking collectives, sent_to_all(): return lax.all_to_all(copies, axis, split_axis=0, concat_axis=0, tiled=True)  10.9 us
    all_to_all x1, starting transfers between devices, per_device(): lax.all_to_all(wanted, 'row', split_axis=0, concat_axis=0, tiled=True)  8.44 us
    reshape x6, local copies, waits for them, and re-layouts, per_device(): arrived = arrived.reshape(seed_count, panel_total * NEED, TILE)  7.81 us
    dot_general x3, matrix products, per_device(): jnp.einsum('mv,emy->evy', indicator_matrix, block_products, precision=lax...  5.89 us
    all_to_all x1, waiting for transfers between devices, per_device(): lax.all_to_all(wanted, 'row', split_axis=0, concat_axis=0, tiled=True)  5.84 us
  transfers between devices with their start and end apart: 2, of which 2 were waited for; matrix products, arithmetic and copies ran while one was open for 1% of the time, Pallas kernels for 0%

commit v1 on v0

v1 whole, which is shorter than its diff:
```python
import functools

import jax
import jax.numpy as jnp
from jax import lax
from jax.experimental import pallas as pl
from jax.experimental.pallas import tpu as pltpu
from jax.sharding import PartitionSpec as P

TILE = 256
NEED = 4
ITERS = 3
CHUNK = 16


def send_blocks(blocks, asked_ref, out_ref):
    for slot in range(out_ref.shape[0]):
        out_ref[slot] = blocks[asked_ref[slot // NEED, slot % NEED]]


def first_pack_kernel(asked_ref, seeds_ref, out_ref, blocks):
    for b in range(blocks.shape[0]):
        blocks[b] = seeds_ref[:, b * TILE:(b + 1) * TILE].astype(jnp.bfloat16)
    send_blocks(blocks, asked_ref, out_ref)


def products(place_ref, row_ref, count_ref, arrived_ref, tiles_ref, tiles_v, acc, sems):
    slots = tiles_ref.shape[0]
    chunks = slots // CHUNK
    copies = []
    for c in range(chunks):
        part = pl.ds(c * CHUNK, CHUNK)
        copies.append(pltpu.make_async_copy(tiles_ref.at[part], tiles_v.at[part], sems.at[c]))
        copies[-1].start()
    acc[...] = jnp.zeros(acc.shape, acc.dtype)
    for c in range(chunks):
        copies[c].wait()

        @pl.when(c * CHUNK < count_ref[0])
        def _():
            for i in range(CHUNK):
                t = c * CHUNK + i
                y = lax.dot_general(
                    arrived_ref[place_ref[t]], tiles_v[t], (((1,), (1,)), ((), ())),
                    preferred_element_type=jnp.float32)
                acc[row_ref[t]] += y


def step_kernel(place_ref, row_ref, count_ref, asked_ref, arrived_ref, decay_ref, seeds_ref, tiles_ref,
                out_ref, tiles_v, acc, blocks, sems):
    products(place_ref, row_ref, count_ref, arrived_ref, tiles_ref, tiles_v, acc, sems)
    decay = decay_ref[...]
    for b in range(blocks.shape[0]):
        x = decay * acc[b] + seeds_ref[:, b * TILE:(b + 1) * TILE]
        blocks[b] = x.astype(jnp.bfloat16)
    send_blocks(blocks, asked_ref, out_ref)


def last_kernel(place_ref, row_ref, count_ref, arrived_ref, decay_ref, seeds_ref, tiles_ref,
                out_ref, squares_ref, tiles_v, acc, sems):
    products(place_ref, row_ref, count_ref, arrived_ref, tiles_ref, tiles_v, acc, sems)
    decay = decay_ref[...]
    total = jnp.zeros((acc.shape[1], 128), jnp.float32)
    for b in range(seeds_ref.shape[1] // TILE):
        x = decay * acc[b] + seeds_ref[:, b * TILE:(b + 1) * TILE]
        out_ref[:, b * TILE:(b + 1) * TILE] = x
        sq = x * x
        total = total + sq[:, :128] + sq[:, 128:]
    squares_ref[...] = jnp.sum(total, axis=1, keepdims=True)


def per_device(tiles, tile_rows, tile_cols, tile_count, seeds, decay):
    slots = tiles.shape[0]
    seed_count = seeds.shape[0]
    blk = seeds.shape[1] // TILE
    panels = lax.axis_size("row")
    bufs = panels * NEED
    live = jnp.arange(slots, dtype=jnp.int32) < tile_count[0]
    owner = tile_cols // blk
    local = tile_cols % blk
    owner_hit = (owner[:, None] == jnp.arange(panels, dtype=jnp.int32)[None, :]) & live[:, None]
    local_hit = local[:, None] == jnp.arange(blk, dtype=jnp.int32)[None, :]
    present = jnp.any(owner_hit[:, :, None] & local_hit[:, None, :], axis=0)
    before = jnp.arange(blk)[:, None] < jnp.arange(blk)[None, :]
    ranking = jnp.sum(jnp.where(present[:, :, None] & before[None], 1, 0), axis=1)
    rank_hit = present[:, :, None] & (ranking[:, :, None] == jnp.arange(NEED)[None, None, :])
    wanted = jnp.sum(jnp.where(rank_hit, jnp.arange(blk, dtype=jnp.int32)[None, :, None], 0), axis=1)
    asked = lax.all_to_all(wanted, "row", split_axis=0, concat_axis=0, tiled=True)
    slot_rank = jnp.sum(jnp.where(owner_hit[:, :, None] & local_hit[:, None, :], ranking[None], 0), axis=(1, 2))
    place = jnp.clip(owner * NEED + slot_rank, 0, bufs - 1)
    row = jnp.where(live, tile_rows, blk)
    decay = decay[:, None]

    smem = pl.BlockSpec(memory_space=pltpu.SMEM)
    vmem = pl.BlockSpec(memory_space=pltpu.VMEM)
    hbm = pl.BlockSpec(memory_space=pl.ANY)
    packed = jax.ShapeDtypeStruct((bufs, seed_count, TILE), jnp.bfloat16)
    blocks = pltpu.VMEM((blk, seed_count, TILE), jnp.bfloat16)
    scratch = [
        pltpu.VMEM(tiles.shape, tiles.dtype),
        pltpu.VMEM((blk + 1, seed_count, TILE), jnp.float32),
    ]
    sems = pltpu.SemaphoreType.DMA((slots // CHUNK,))
    params = pltpu.CompilerParams(vmem_limit_bytes=24 * 1024 * 1024)

    outgoing = pl.pallas_call(
        first_pack_kernel, out_shape=packed, in_specs=[smem, vmem], out_specs=vmem,
        scratch_shapes=[blocks], compiler_params=params, name="first_pack")(asked, seeds)
    for step in range(ITERS):
        arrived = lax.all_to_all(outgoing, "row", split_axis=0, concat_axis=0, tiled=True)
        if step < ITERS - 1:
            outgoing = pl.pallas_call(
                step_kernel, out_shape=packed, in_specs=[smem, smem, smem, smem, vmem, vmem, vmem, hbm], out_specs=vmem,
                scratch_shapes=scratch + [blocks, sems], compiler_params=params, name="step",
            )(place, row, tile_count, asked, arrived, decay, seeds, tiles)
        else:
            iterate, squares = pl.pallas_call(
                last_kernel,
                out_shape=(jax.ShapeDtypeStruct(seeds.shape, jnp.float32), jax.ShapeDtypeStruct((seed_count, 1), jnp.float32)),
                in_specs=[smem, smem, smem, vmem, vmem, vmem, hbm], out_specs=(vmem, vmem),
                scratch_shapes=scratch + [sems], compiler_params=params, name="last",
            )(place, row, tile_count, arrived, decay, seeds, tiles)
    copies = jnp.broadcast_to(squares.reshape(1, 1, seed_count), (panels, 1, seed_count))
    squares = jnp.sum(lax.all_to_all(copies, "row", split_axis=0, concat_axis=0, tiled=True), axis=(0, 1))
    norm_value = jnp.sqrt(squares / (panels * iterate.shape[1]) + 1e-06)
    return iterate / norm_value[:, None]


def solution(mesh):
    in_specs = (
        P(("graph", "row"), None, None),
        P(("graph", "row")),
        P(("graph", "row")),
        P(("graph", "row")),
        P(None, ("graph", "row")),
        P(),
    )
    return jax.shard_map(
        per_device, mesh=mesh, in_specs=in_specs, out_specs=P(None, ("graph", "row")), check_vma=False)
```

time: 139 us -> 112 us (0.81)
  matrix products: 23.8 us -> 0 us
  blocking collectives: 51.4 us -> 73.3 us
  local copies, waits for them, and re-layouts: 22.8 us -> 6.3 us
  Pallas kernels: 0 us -> 8.45 us
  starting transfers between devices: 12.5 us -> 4.11 us
  waiting for transfers between devices: 22.4 us -> 15.8 us
  other arithmetic: 4.73 us -> 3.15 us
    dot_general x7 -> x0, matrix products: 23.8 us -> none  [the longest x3 17.7 us: per_device(): jnp.einsum('trc,stc->str', tiles, picked, preferred_element_type=jnp.floa...]
    all_to_all x3 -> x4, blocking collectives: 51.4 us -> 73.3 us  [the longest x2 45 us: per_device(): lax.all_to_all(outgoing, 'row', split_axis=0, concat_axis=0, tiled=True)]
    reshape x16 -> x0, local copies, waits for them, and re-layouts: 12.7 us -> none  [the longest x6 7.81 us: per_device(): arrived = arrived.reshape(seed_count, panel_total * NEED, TILE)]
    pallas_call x0 -> x4, Pallas kernels: none -> 8.45 us  [the longest x2 4.54 us: per_device(): pl.pallas_call(step_kernel, out_shape=packed, in_specs=[smem, smem, smem,...]
    all_to_all x2 -> x1, starting transfers between devices: 12.5 us -> 4.11 us  [per_device(): lax.all_to_all(outgoing, 'row', split_axis=0, concat_axis=0, tiled=True)]
    all_to_all x2 -> x1, waiting for transfers between devices: 22.4 us -> 15.8 us  [per_device(): lax.all_to_all(outgoing, 'row', split_axis=0, concat_axis=0, tiled=True)]
    unnamed x9 -> x10, local copies, waits for them, and re-layouts: 0.95 us -> 5.47 us
    gather x7 -> x0, local copies, waits for them, and re-layouts: 4.49 us -> none  [the longest x3 1.85 us: per_device(): jnp.take(own_blocks, asked_flat, axis=1)]
  transfers between devices with their start and end apart: 2 -> 1, of which waited for: 2 -> 1; matrix products, arithmetic and copies ran while one was open for 1% -> 1% of each run, Pallas kernels for 0% -> 0%
where the time goes in v1:
time: 112 us
  blocking collectives  73.3 us (65%)
  waiting for transfers between devices  15.8 us (14%)
  Pallas kernels  8.45 us (8%)
  local copies, waits for them, and re-layouts  6.3 us (6%)
  starting transfers between devices  4.11 us (4%)
  other arithmetic  3.15 us (3%)
    all_to_all x2, blocking collectives, per_device(): lax.all_to_all(outgoing, 'row', split_axis=0, concat_axis=0, tiled=True)  45 us
    all_to_all x1, waiting for transfers between devices, per_device(): lax.all_to_all(outgoing, 'row', split_axis=0, concat_axis=0, tiled=True)  15.8 us
    all_to_all x1, blocking collectives, per_device(): lax.all_to_all(wanted, 'row', split_axis=0, concat_axis=0, tiled=True)  15.2 us
    all_to_all x1, blocking collectives, per_device(): lax.all_to_all(copies, 'row', split_axis=0, concat_axis=0, tiled=True)  13.1 us
    unnamed x10, local copies, waits for them, and re-layouts  5.47 us
    pallas_call x2, Pallas kernels, per_device(): pl.pallas_call(step_kernel, out_shape=packed, in_specs=[smem, smem, smem,...  4.54 us
    all_to_all x1, starting transfers between devices, per_device(): lax.all_to_all(outgoing, 'row', split_axis=0, concat_axis=0, tiled=True)  4.11 us
  transfers between devices with their start and end apart: 1, of which 1 were waited for; matrix products, arithmetic and copies ran while one was open for 1% of the time, Pallas kernels for 0%

profile of v1, /device:TPU:1, one launch (start us, length us, event | category | flops | bytes accessed | tf_op | source)
XLA Modules:
  0.0 111.9 jit_solution(9542788917205759074)
XLA Ops:
  0.7 0.7 and_select_fusion.2
  1.4 0.4 and_reduce_fusion
  1.7 0.1 select_reduce_fusion
  1.8 0.1 select_reduce_fusion.1
  2.0 0.1 copy.35
  2.1 15.2 %all_to_all.31 = s32[16,1,4]{2,1,0:T(1,128)S(1)} all-to-all(s32[16,1,4]{2,1,0:T(1,128)S(1)} %copy.35), channel_id=1, replica_groups=mesh['graph'=16,'row'=16] {'row'}, dimensions={0} | all-to-all | bytes 512 | tf_op jit(solution)/shard_map/all_to_all | solution.py:88
  17.3 0.0 copy-start.2
  17.3 1.0 copy-done.2
  18.4 1.8 %first_pack.1 = bf16[64,32,256]{2,1,0:T(8,128)(2,1)} custom-call(s32[16,4]{1,0:T(8,128)S(1)} %bitcast.7, f32[32,4096]{1,0:T(8,128)S(1)} %copy-done.2), custom_call_target="tpu_custom_call" | custom-call | tf_op jit(solution)/shard_map/first_pack/pallas_call | solution.py:106
  20.1 4.1 %all-to-all-start.1 = ((bf16[64,32,256]{2,1,0:T(8,128)(2,1)}), bf16[64,32,256]{2,1,0:T(8,128)(2,1)S(1)}, u32[]{:S(2)}, u32[]{:S(2)}) async-start(bf16[64,32,256]{2,1,0:T(8,128)(2,1)} %first_pack.1), calls=%async_computation.1 | async-start | bytes 2097152 | tf_op jit(solution)/shard_map/all_to_all | solution.py:110
  24.2 0.7 copy.39.decay_ref
  25.0 0.1 fusion
  25.1 0.7 broadcast_select_fusion.row_ref
  25.7 15.8 %all-to-all-done.1.arrived_ref = bf16[64,32,256]{2,1,0:T(8,128)(2,1)S(1)} async-done(((bf16[64,32,256]{2,1,0:T(8,128)(2,1)}), bf16[64,32,256]{2,1,0:T(8,128)(2,1)S(1)}, u32[]{:S(2)}, u32[]{:S(2)}) %all-to-all-start.1) | async-done | bytes 1048608 | tf_op jit(solution)/shard_map/all_to_all | solution.py:110
  41.6 0.0 copy-start
  41.6 3.4 %copy-done = bf16[64,256,256]{2,1,0:T(8,128)(2,1)S(1)} copy-done((bf16[64,256,256]{2,1,0:T(8,128)(2,1)S(1)}, bf16[64,256,256]{2,1,0:T(8,128)(2,1)}, u32[]{:S(2)}) %copy-start) | copy-done | bytes 8388632
  45.0 0.0 copy-start.3
  45.0 1.0 copy-done.3
  46.0 0.0 copy-start.1
  46.0 2.3 %step.2 = bf16[64,32,256]{2,1,0:T(8,128)(2,1)S(1)} custom-call(s32[64]{0:T(128)S(1)} %add_clamp_fusion.place_ref, s32[64]{0:T(128)S(1)} %broadcast_select_fusion.row_ref, s32[1]{0:T(128)} %copy.45.count_ref, s32[16,4]{1,0:T(8,128)S(1)} %bitcast.8, bf16[64,32,256]{2,1,0:T(8,128)(2,1)S(1)} %all-to-all-done.1.arrived_ref, f32[32,1]{1,0:T(8,128)S(1)} %copy.39.decay_ref, ...), custom_call_target="tpu_custom_call" | custom-call | tf_op jit(solution)/shard_map/step/pallas_call | solution.py:112
  48.3 0.0 copy-start.4
  48.3 22.2 %all_to_all.32.arrived_ref = bf16[64,32,256]{2,1,0:T(8,128)(2,1)S(1)} all-to-all(bf16[64,32,256]{2,1,0:T(8,128)(2,1)S(1)} %step.2), channel_id=1, replica_groups=mesh['graph'=16,'row'=16] {'row'}, dimensions={0} | all-to-all | bytes 2097152 | tf_op jit(solution)/shard_map/all_to_all | solution.py:110
  70.5 0.0 copy-done.1
  70.5 2.3 %step.3 = bf16[64,32,256]{2,1,0:T(8,128)(2,1)S(1)} custom-call(s32[64]{0:T(128)S(1)} %add_clamp_fusion.place_ref, s32[64]{0:T(128)S(1)} %broadcast_select_fusion.row_ref, s32[1]{0:T(128)} %copy.45.count_ref, s32[16,4]{1,0:T(8,128)S(1)} %bitcast.9, bf16[64,32,256]{2,1,0:T(8,128)(2,1)S(1)} %all_to_all.32.arrived_ref, f32[32,1]{1,0:T(8,128)S(1)} %copy.39.decay_ref, ...), custom_call_target="tpu_custom_call" | custom-call | tf_op jit(solution)/shard_map/step/pallas_call | solution.py:112
  72.8 22.8 %all_to_all.33.arrived_ref = bf16[64,32,256]{2,1,0:T(8,128)(2,1)S(1)} all-to-all(bf16[64,32,256]{2,1,0:T(8,128)(2,1)S(1)} %step.3), channel_id=1, replica_groups=mesh['graph'=16,'row'=16] {'row'}, dimensions={0} | all-to-all | bytes 2097152 | tf_op jit(solution)/shard_map/all_to_all | solution.py:110
  95.6 0.0 copy-done.4
  95.6 2.2 %last.1 = (f32[32,4096]{1,0:T(8,128)S(1)}, f32[32,1]{1,0:T(8,128)S(1)}) custom-call(s32[64]{0:T(128)S(1)} %add_clamp_fusion.place_ref, s32[64]{0:T(128)S(1)} %broadcast_select_fusion.row_ref, s32[1]{0:T(128)} %copy.45.count_ref, bf16[64,32,256]{2,1,0:T(8,128)(2,1)S(1)} %all_to_all.33.arrived_ref, f32[32,1]{1,0:T(8,128)S(1)} %copy.39.decay_ref, ...), custom_call_target="tpu_custom_call" | custom-call | tf_op jit(solution)/shard_map/last/pallas_call | solution.py:117
  97.8 0.1 reduce
  97.9 13.1 %all_to_all.34 = f32[16,1,32]{2,1,0:T(1,128)S(1)} all-to-all(f32[16,1,32]{2,1,0:T(1,128)S(1)} %broadcast_in_dim.71), channel_id=1, replica_groups=mesh['graph'=16,'row'=16] {'row'}, dimensions={0} | all-to-all | bytes 4096 | tf_op jit(solution)/shard_map/all_to_all | solution.py:124
  111.0 0.9 broadcast_divide_fusion
  (7 shorter events, 0.1 us)
Async XLA Ops:
  17.3 1.0 copy-start.2
  20.1 21.5 %all-to-all-start.1 = ((bf16[64,32,256]{2,1,0:T(8,128)(2,1)}), bf16[64,32,256]{2,1,0:T(8,128)(2,1)S(1)}, u32[]{:S(2)}, u32[]{:S(2)}) async-start(bf16[64,32,256]{2,1,0:T(8,128)(2,1)} %first_pack.1), calls=%async_computation.1 | async-start | bytes 2097152 | tf_op jit(solution)/shard_map/all_to_all | solution.py:110
  41.6 3.4 %copy-start = (bf16[64,256,256]{2,1,0:T(8,128)(2,1)S(1)}, bf16[64,256,256]{2,1,0:T(8,128)(2,1)}, u32[]{:S(2)}) copy-start(bf16[64,256,256]{2,1,0:T(8,128)(2,1)} %tiles_ref.5) | copy-start | bytes 25165828
  45.0 1.0 copy-start.3
  46.0 24.5 %copy-start.1 = (bf16[64,256,256]{2,1,0:T(8,128)(2,1)S(1)}, bf16[64,256,256]{2,1,0:T(8,128)(2,1)}, u32[]{:S(2)}) copy-start(bf16[64,256,256]{2,1,0:T(8,128)(2,1)} %tiles_ref.5) | copy-start | bytes 25165828
  48.3 47.3 %copy-start.4 = (f32[32,4096]{1,0:T(8,128)S(1)}, f32[32,4096]{1,0:T(8,128)}, u32[]{:S(2)}) copy-start(f32[32,4096]{1,0:T(8,128)} %seeds_ref.7) | copy-start | bytes 1572868

commit v2 on v1

v2 whole, which is shorter than its diff:
```python
import functools

import jax
import jax.numpy as jnp
from jax import lax
from jax.experimental import pallas as pl
from jax.experimental.pallas import tpu as pltpu
from jax.sharding import PartitionSpec as P

TILE = 256
NEED = 4
ITERS = 3


def in_hbm(x):
    return pltpu.with_memory_space_constraint(x, pltpu.HBM)


def index_kernel(count_ref, cols_ref, rows_ref, decay_ref, seeds_ref, wanted_ref, place_ref, row_ref, column_ref,
                 rounded_ref, cols_v, rows_v, decay_v, seeds_v, sems):
    blk = rounded_ref.shape[0]
    panels = wanted_ref.shape[0]
    slots = cols_v.shape[1]
    seed_count = seeds_v.shape[0]
    gets = []
    for i, (src, dst) in enumerate(((cols_ref, cols_v), (rows_ref, rows_v), (decay_ref, decay_v), (seeds_ref, seeds_v))):
        gets.append(pltpu.make_async_copy(src, dst, sems.at[i]))
        gets[-1].start()
    gets[0].wait()
    live = lax.broadcasted_iota(jnp.int32, (panels, slots), 1) < count_ref[0]
    panel = lax.broadcasted_iota(jnp.int32, (panels, slots), 0)
    local = jnp.where(live, cols_v[...] - blk * panel, -1)
    rank = jnp.zeros((panels, 1), jnp.float32)
    picks = [jnp.zeros((panels, 1), jnp.float32) for _ in range(NEED)]
    spot = jnp.zeros((panels, slots), jnp.float32)
    first = (NEED * panel).astype(jnp.float32)
    for b in range(blk):
        hit = local == b
        spot = jnp.where(hit, first + rank, spot)
        here = jnp.max(jnp.where(hit, 1.0, 0.0), axis=1, keepdims=True)
        for k in range(NEED):
            picks[k] = jnp.where((here > 0) & (rank == k), float(b), picks[k])
        rank = rank + here
    lane = lax.broadcasted_iota(jnp.int32, (panels, NEED), 1)
    wanted = jnp.zeros((panels, NEED), jnp.float32)
    for k in range(NEED):
        wanted = jnp.where(lane == k, picks[k], wanted)
    wanted = wanted.astype(jnp.int32)
    for q in range(panels):
        wanted_ref[q] = wanted[q:q + 1]
    place_ref[...] = jnp.sum(spot, axis=0, keepdims=True).astype(jnp.int32)
    gets[1].wait()
    row_ref[...] = jnp.where(live[:1], rows_v[...], blk)
    gets[2].wait()
    column_ref[...] = to_column(decay_v[...], seed_count)
    gets[3].wait()
    for b in range(blk):
        rounded_ref[b] = seeds_v[:, b * TILE:(b + 1) * TILE].astype(jnp.bfloat16)


def to_column(x, size):
    square = (size, size)
    diagonal = lax.broadcasted_iota(jnp.int32, square, 0) == lax.broadcasted_iota(jnp.int32, square, 1)
    return jnp.sum(jnp.where(diagonal, jnp.broadcast_to(x, square), 0.0), axis=1, keepdims=True)


def send_blocks(blocks, asked_ref, out_ref):
    for slot in range(out_ref.shape[0]):
        out_ref[slot] = blocks[asked_ref[slot // NEED, slot % NEED]]


def first_pack_kernel(asked_ref, rounded_ref, out_ref):
    send_blocks(rounded_ref, asked_ref, out_ref)


def products(place_ref, row_ref, arrived_ref, tiles_ref, acc, turned_ref=None):
    acc[...] = jnp.zeros(acc.shape, acc.dtype)
    for t in range(tiles_ref.shape[0]):
        x = arrived_ref[place_ref[0, t]]
        if turned_ref is None:
            y = jnp.dot(x, tiles_ref[t], preferred_element_type=jnp.float32)
        else:
            tile = tiles_ref[t]
            turned_ref[t] = tile.T
            y = lax.dot_general(x, tile, (((1,), (1,)), ((), ())), preferred_element_type=jnp.float32)
        acc[row_ref[0, t]] += y


def update(asked_ref, decay_ref, seeds_ref, out_ref, acc, blocks):
    decay = decay_ref[...]
    for b in range(blocks.shape[0]):
        blocks[b] = (decay * acc[b] + seeds_ref[:, b * TILE:(b + 1) * TILE]).astype(jnp.bfloat16)
    send_blocks(blocks, asked_ref, out_ref)


def turn_step_kernel(place_ref, row_ref, asked_ref, arrived_ref, decay_ref, seeds_ref, tiles_ref,
                     out_ref, turned_ref, acc, blocks):
    products(place_ref, row_ref, arrived_ref, tiles_ref, acc, turned_ref)
    update(asked_ref, decay_ref, seeds_ref, out_ref, acc, blocks)


def step_kernel(place_ref, row_ref, asked_ref, arrived_ref, decay_ref, seeds_ref, tiles_ref, out_ref, acc, blocks):
    products(place_ref, row_ref, arrived_ref, tiles_ref, acc)
    update(asked_ref, decay_ref, seeds_ref, out_ref, acc, blocks)


def last_kernel(place_ref, row_ref, arrived_ref, decay_ref, seeds_ref, tiles_ref, out_ref, squares_ref, acc):
    products(place_ref, row_ref, arrived_ref, tiles_ref, acc)
    decay = decay_ref[...]
    total = jnp.zeros((acc.shape[1], 128), jnp.float32)
    for b in range(seeds_ref.shape[1] // TILE):
        x = decay * acc[b] + seeds_ref[:, b * TILE:(b + 1) * TILE]
        out_ref[:, b * TILE:(b + 1) * TILE] = x
        sq = x * x
        total = total + sq[:, :128] + sq[:, 128:]
    squares_ref[...] = jnp.broadcast_to(jnp.sum(total.T, axis=0, keepdims=True)[None], squares_ref.shape)


def scale_kernel(squares_ref, iterate_ref, out_ref, buf, sems):
    seed_count, nodes = iterate_ref.shape
    panels = squares_ref.shape[0]
    total = squares_ref[0]
    for p in range(1, panels):
        total = total + squares_ref[p]
    factor = to_column(1.0 / jnp.sqrt(total / (panels * nodes) + 1e-06), seed_count)
    puts = []
    parts = sems.shape[0]
    for c in range(parts):
        part = pl.ds(c * nodes // parts, nodes // parts)
        buf[:, part] = iterate_ref[:, part] * factor
        puts.append(pltpu.make_async_copy(buf.at[:, part], out_ref.at[:, part], sems.at[c]))
        puts[-1].start()
    for put in puts:
        put.wait()


def per_device(tiles, tile_rows, tile_cols, tile_count, seeds, decay):
    slots = tiles.shape[0]
    seed_count = seeds.shape[0]
    blk = seeds.shape[1] // TILE
    panels = lax.axis_size("row")
    bufs = panels * NEED
    smem = pl.BlockSpec(memory_space=pltpu.SMEM)
    vmem = pl.BlockSpec(memory_space=pltpu.VMEM)
    hbm = pl.BlockSpec(memory_space=pltpu.HBM)
    dma = pltpu.SemaphoreType.DMA
    mib = 1024 * 1024
    packed = jax.ShapeDtypeStruct((bufs, seed_count, TILE), jnp.bfloat16)
    blocks_shape = (blk, seed_count, TILE)
    blocks = pltpu.VMEM(blocks_shape, jnp.bfloat16)
    acc = pltpu.VMEM((blk + 1, seed_count, TILE), jnp.float32)
    seeds_v = pltpu.VMEM(seeds.shape, seeds.dtype)
    small = pltpu.CompilerParams(vmem_limit_bytes=6 * mib)

    f32, i32 = jnp.float32, jnp.int32
    shape = jax.ShapeDtypeStruct
    wanted, place, row, column, rounded = pl.pallas_call(
        index_kernel,
        out_shape=(shape((panels, 1, NEED), i32), shape((1, slots), i32), shape((1, slots), i32),
                   shape((seed_count, 1), f32), shape(blocks_shape, jnp.bfloat16)),
        in_specs=[smem, hbm, hbm, hbm, hbm], out_specs=(vmem,) * 5,
        scratch_shapes=[pltpu.VMEM((1, slots), i32), pltpu.VMEM((1, slots), i32), pltpu.VMEM((1, seed_count), f32),
                        seeds_v, dma((4,))],
        compiler_params=small, name="index",
    )(tile_count, in_hbm(tile_cols.reshape(1, slots)), in_hbm(tile_rows.reshape(1, slots)),
      in_hbm(decay.reshape(1, seed_count)), in_hbm(seeds))
    asked = lax.all_to_all(wanted, "row", split_axis=0, concat_axis=0, tiled=True).reshape(panels, NEED)
    outgoing = pl.pallas_call(
        first_pack_kernel, out_shape=packed, in_specs=[smem, vmem], out_specs=vmem,
        compiler_params=small, name="first_pack",
        cost_estimate=pl.CostEstimate(flops=20_000_000_000, bytes_accessed=2 * mib, transcendentals=0))(asked, rounded)

    for step in range(ITERS):
        arrived = lax.all_to_all(outgoing, "row", split_axis=0, concat_axis=0, tiled=True)
        if step == 0:
            outgoing, turned = pl.pallas_call(
                turn_step_kernel, out_shape=(packed, shape(tiles.shape, tiles.dtype)),
                in_specs=[smem, smem, smem, vmem, vmem, vmem, vmem], out_specs=(vmem, vmem),
                scratch_shapes=[acc, blocks], compiler_params=small, name="turn_step",
            )(place, row, asked, arrived, column, seeds, tiles)
        elif step < ITERS - 1:
            outgoing = pl.pallas_call(
                step_kernel, out_shape=packed, in_specs=[smem, smem, smem, vmem, vmem, vmem, vmem], out_specs=vmem,
                scratch_shapes=[acc, blocks], compiler_params=small, name="step",
            )(place, row, asked, arrived, column, seeds, turned)
        else:
            iterate, squares = pl.pallas_call(
                last_kernel, out_shape=(shape(seeds.shape, f32), shape((panels, 1, seed_count), f32)),
                in_specs=[smem, smem, vmem, vmem, vmem, vmem], out_specs=(vmem, vmem),
                scratch_shapes=[acc], compiler_params=small, name="last",
            )(place, row, arrived, column, seeds, turned)
    squares = lax.all_to_all(squares, "row", split_axis=0, concat_axis=0, tiled=True)
    return pl.pallas_call(
        scale_kernel, out_shape=shape(seeds.shape, f32), in_specs=[vmem, vmem], out_specs=hbm,
        scratch_shapes=[seeds_v, dma((4,))], compiler_params=small, name="scale")(squares, iterate)


def solution(mesh):
    in_specs = (
        P(("graph", "row"), None, None),
        P(("graph", "row")),
        P(("graph", "row")),
        P(("graph", "row")),
        P(None, ("graph", "row")),
        P(),
    )
    return jax.shard_map(
        per_device, mesh=mesh, in_specs=in_specs, out_specs=P(None, ("graph", "row")), check_vma=False)
```

time: 112 us -> 99.4 us (0.89)
  waiting for transfers between devices: 15.8 us -> 0 us
  blocking collectives: 73.3 us -> 87.5 us
  local copies, waits for them, and re-layouts: 6.3 us -> 0.01 us
  starting transfers between devices: 4.11 us -> 0 us
  other arithmetic: 3.15 us -> 0 us
  Pallas kernels: 8.45 us -> 10.9 us
    all_to_all x2 -> x3, blocking collectives: 45 us -> 61.4 us  [per_device(): lax.all_to_all(outgoing, 'row', split_axis=0, concat_axis=0, tiled=True)]
    all_to_all x1 -> x0, waiting for transfers between devices: 15.8 us -> none  [per_device(): lax.all_to_all(outgoing, 'row', split_axis=0, concat_axis=0, tiled=True)]
    pallas_call x1 -> x4, Pallas kernels: 2.16 us -> 7.84 us  [the longest x1 3.42 us: per_device(): pl.pallas_call(turn_step_kernel, out_shape=(packed, shape(tiles.shape, ti...]
    unnamed x10 -> x4, local copies, waits for them, and re-layouts: 5.47 us -> 0.01 us
    all_to_all x1 -> x0, starting transfers between devices: 4.11 us -> none  [per_device(): lax.all_to_all(outgoing, 'row', split_axis=0, concat_axis=0, tiled=True)]
    pallas_call x2 -> x1, Pallas kernels: 4.54 us -> 2.35 us  [per_device(): pl.pallas_call(step_kernel, out_shape=packed, in_specs=[smem, smem, smem,...]
    all_to_all x1, blocking collectives: 13.1 us -> 10.9 us  [per_device(): lax.all_to_all(squares, 'row', split_axis=0, concat_axis=0, tiled=True)]
    select_n x2 -> x0, other arithmetic: 1.33 us -> none  [the longest x1 0.67 us: per_device(): owner = tile_cols // blk]
  transfers between devices with their start and end apart: 1 -> 0, of which waited for: 1 -> 0; matrix products, arithmetic and copies ran while one was open for 1% -> 0% of each run, Pallas kernels for 0% -> 0%
where the time goes in v2:
time: 99.4 us; the launch traced here: 99.1 us
  blocking collectives  87.5 us (88%)
  Pallas kernels  10.9 us (11%)
    all_to_all x3, blocking collectives, per_device(): lax.all_to_all(outgoing, 'row', split_axis=0, concat_axis=0, tiled=True)  61.4 us
    all_to_all x1, blocking collectives, per_device(): lax.all_to_all(wanted, 'row', split_axis=0, concat_axis=0, tiled=True)  15.2 us
    all_to_all x1, blocking collectives, per_device(): lax.all_to_all(squares, 'row', split_axis=0, concat_axis=0, tiled=True)  10.9 us
    pallas_call x1, Pallas kernels, per_device(): pl.pallas_call(turn_step_kernel, out_shape=(packed, shape(tiles.shape, ti...  3.42 us
    pallas_call x1, Pallas kernels, per_device(): pl.pallas_call(step_kernel, out_shape=packed, in_specs=[smem, smem, smem,...  2.35 us
    pallas_call x1, Pallas kernels, per_device(): pl.pallas_call(last_kernel, out_shape=(shape(seeds.shape, f32), shape((pa...  2.31 us

profile of v2, /device:TPU:1, one launch (start us, length us, event | category | flops | bytes accessed | tf_op | source)
XLA Modules:
  0.0 99.1 jit_solution(3465491781700933996)
XLA Ops:
  0.7 1.2 %index.1 = (s32[16,1,4]{2,1,0:T(1,128)S(1)}, s32[1,64]{1,0:T(1,128)S(1)}, s32[1,64]{1,0:T(1,128)S(1)}, f32[32,1]{1,0:T(8,128)S(1)}, bf16[16,32,256]{2,1,0:T(8,128)(2,1)S(1)}) custom-call(s32[1]{0:T(128)S(6)} %copy.12.count_ref, s32[1,64]{1,0:T(1,128)} %bitcast.7, s32[1,64]{1,0:T(1,128)} %bitcast.8, f32[1,32]{1,0:T(1,128)} %bitcast.9, f32[32,4096]{1,0:T(8,128)} %seeds_ref.7), custom_call_target="tpu_custom_call" | custom-call | tf_op jit(solution)/shard_map/index/pallas_call | solution.py:157
  1.8 15.2 %all_to_all.25 = s32[16,1,4]{2,1,0:T(1,128)S(1)} all-to-all(s32[16,1,4]{2,1,0:T(1,128)S(1)} %get-tuple-element.16), channel_id=1, replica_groups=mesh['graph'=16,'row'=16] {'row'}, dimensions={0} | all-to-all | bytes 512 | tf_op jit(solution)/shard_map/all_to_all | solution.py:167
  17.1 0.0 copy-start
  17.1 0.0 copy-start.1
  17.1 0.7 first_pack.1
  17.8 20.2 %all_to_all.26.arrived_ref = bf16[64,32,256]{2,1,0:T(8,128)(2,1)S(1)} all-to-all(bf16[64,32,256]{2,1,0:T(8,128)(2,1)S(1)} %first_pack.1), channel_id=1, replica_groups=mesh['graph'=16,'row'=16] {'row'}, dimensions={0} | all-to-all | bytes 2097152 | tf_op jit(solution)/shard_map/all_to_all | solution.py:174
  38.0 0.0 copy-done
  38.0 0.0 copy-done.1
  38.0 3.4 %turn_step.1 = (bf16[64,32,256]{2,1,0:T(8,128)(2,1)S(1)}, bf16[64,256,256]{2,1,0:T(8,128)(2,1)S(1)}) custom-call(s32[1,64]{1,0:T(1,128)S(1)} %get-tuple-element.14.place_ref, s32[1,64]{1,0:T(1,128)S(1)} %get-tuple-element.15.row_ref, s32[16,4]{1,0:T(8,128)S(1)} %bitcast.5, bf16[64,32,256]{2,1,0:T(8,128)(2,1)S(1)} %all_to_all.26.arrived_ref, ...), custom_call_target="tpu_custom_call" | custom-call | tf_op jit(solution)/shard_map/turn_step/pallas_call | solution.py:176
  41.5 20.6 %all_to_all.27.arrived_ref = bf16[64,32,256]{2,1,0:T(8,128)(2,1)S(1)} all-to-all(bf16[64,32,256]{2,1,0:T(8,128)(2,1)S(1)} %get-tuple-element.19), channel_id=1, replica_groups=mesh['graph'=16,'row'=16] {'row'}, dimensions={0} | all-to-all | bytes 2097152 | tf_op jit(solution)/shard_map/all_to_all | solution.py:174
  62.0 2.4 %step.1 = bf16[64,32,256]{2,1,0:T(8,128)(2,1)S(1)} custom-call(s32[1,64]{1,0:T(1,128)S(1)} %get-tuple-element.14.place_ref, s32[1,64]{1,0:T(1,128)S(1)} %get-tuple-element.15.row_ref, s32[16,4]{1,0:T(8,128)S(1)} %bitcast.6, bf16[64,32,256]{2,1,0:T(8,128)(2,1)S(1)} %all_to_all.27.arrived_ref, f32[32,1]{1,0:T(8,128)S(1)} %get-tuple-element.18.decay_ref, ...), custom_call_target="tpu_custom_call" | custom-call | tf_op jit(solution)/shard_map/step/pallas_call | solution.py:182
  64.4 20.6 %all_to_all.28.arrived_ref = bf16[64,32,256]{2,1,0:T(8,128)(2,1)S(1)} all-to-all(bf16[64,32,256]{2,1,0:T(8,128)(2,1)S(1)} %step.1), channel_id=1, replica_groups=mesh['graph'=16,'row'=16] {'row'}, dimensions={0} | all-to-all | bytes 2097152 | tf_op jit(solution)/shard_map/all_to_all | solution.py:174
  85.0 2.3 %last.1 = (f32[32,4096]{1,0:T(8,128)S(1)}, f32[16,1,32]{2,1,0:T(1,128)S(1)}) custom-call(s32[1,64]{1,0:T(1,128)S(1)} %get-tuple-element.14.place_ref, s32[1,64]{1,0:T(1,128)S(1)} %get-tuple-element.15.row_ref, bf16[64,32,256]{2,1,0:T(8,128)(2,1)S(1)} %all_to_all.28.arrived_ref, f32[32,1]{1,0:T(8,128)S(1)} %get-tuple-element.18.decay_ref, ...), custom_call_target="tpu_custom_call" | custom-call | tf_op jit(solution)/shard_map/last/pallas_call | solution.py:187
  87.3 10.9 %all_to_all.29.squares_ref = f32[16,1,32]{2,1,0:T(1,128)S(1)} all-to-all(f32[16,1,32]{2,1,0:T(1,128)S(1)} %get-tuple-element.21), channel_id=1, replica_groups=mesh['graph'=16,'row'=16] {'row'}, dimensions={0} | all-to-all | bytes 4096 | tf_op jit(solution)/shard_map/all_to_all | solution.py:192
  98.2 0.9 scale.1
Async XLA Ops:
  17.1 21.0 %copy-start = (f32[32,4096]{1,0:T(8,128)S(1)}, f32[32,4096]{1,0:T(8,128)}, u32[]{:S(2)}) copy-start(f32[32,4096]{1,0:T(8,128)} %seeds_ref.7) | copy-start | bytes 1572868
  17.1 21.0 %copy-start.1 = (bf16[64,256,256]{2,1,0:T(8,128)(2,1)S(1)}, bf16[64,256,256]{2,1,0:T(8,128)(2,1)}, u32[]{:S(2)}) copy-start(bf16[64,256,256]{2,1,0:T(8,128)(2,1)} %tiles_ref.1) | copy-start | bytes 25165828

commit v3 on v2

--- a/solution.py
+++ b/solution.py
@@ -16,10 +16,11 @@
     return pltpu.with_memory_space_constraint(x, pltpu.HBM)
 
 
-def index_kernel(count_ref, cols_ref, rows_ref, decay_ref, seeds_ref, wanted_ref, place_ref, row_ref, column_ref,
+def index_kernel(count_ref, half_ref, cols_ref, rows_ref, decay_ref, seeds_ref, wanted_ref, near_place_ref, place_ref, row_ref, column_ref,
                  rounded_ref, cols_v, rows_v, decay_v, seeds_v, sems):
     blk = rounded_ref.shape[0]
     panels = wanted_ref.shape[0]
+    group = panels // 2
     slots = cols_v.shape[1]
     seed_count = seeds_v.shape[0]
     gets = []
@@ -41,14 +42,19 @@
         for k in range(NEED):
             picks[k] = jnp.where((here > 0) & (rank == k), float(b), picks[k])
         rank = rank + here
-    lane = lax.broadcasted_iota(jnp.int32, (panels, NEED), 1)
-    wanted = jnp.zeros((panels, NEED), jnp.float32)
+    lane = lax.broadcasted_iota(jnp.int32, (panels, 2 * NEED), 1)
+    wanted = jnp.zeros((panels, 2 * NEED), jnp.float32)
     for k in range(NEED):
-        wanted = jnp.where(lane == k, picks[k], wanted)
+        partner = jnp.concatenate([picks[k][group:], picks[k][:group]], axis=0)
+        wanted = jnp.where(lane == k, picks[k], jnp.where(lane == NEED + k, partner, wanted))
     wanted = wanted.astype(jnp.int32)
     for q in range(panels):
         wanted_ref[q] = wanted[q:q + 1]
     place_ref[...] = jnp.sum(spot, axis=0, keepdims=True).astype(jnp.int32)
+    side = jnp.where((panel >= group) == (half_ref[0] == 1), 0, NEED)
+    shift = ((panel % group) * 2 * NEED + side - panel * NEED).astype(jnp.float32)
+    near_spot = jnp.where(local >= 0, jnp.where(local < blk, spot + shift, 0.0), 0.0)
+    near_place_ref[...] = jnp.sum(near_spot, axis=0, keepdims=True).astype(jnp.int32)
     gets[1].wait()
     row_ref[...] = jnp.where(live[:1], rows_v[...], blk)
     gets[2].wait()
@@ -64,13 +70,18 @@
     return jnp.sum(jnp.where(diagonal, jnp.broadcast_to(x, square), 0.0), axis=1, keepdims=True)
 
 
+def first_pack_kernel(half_ref, asked_ref, rounded_ref, other_ref, out_ref):
+    group = asked_ref.shape[0] // 2
+    for g in range(group):
+        q = half_ref[0] * group + g
+        for k in range(NEED):
+            out_ref[2 * NEED * g + k] = rounded_ref[asked_ref[q, k]]
+            out_ref[2 * NEED * g + NEED + k] = other_ref[asked_ref[q, NEED + k]]
+
+
 def send_blocks(blocks, asked_ref, out_ref):
     for slot in range(out_ref.shape[0]):
         out_ref[slot] = blocks[asked_ref[slot // NEED, slot % NEED]]
-
-
-def first_pack_kernel(asked_ref, rounded_ref, out_ref):
-    send_blocks(rounded_ref, asked_ref, out_ref)
 
 
 def products(place_ref, row_ref, arrived_ref, tiles_ref, acc, turned_ref=None):
@@ -99,7 +110,8 @@
     update(asked_ref, decay_ref, seeds_ref, out_ref, acc, blocks)
 
 
-def step_kernel(place_ref, row_ref, asked_ref, arrived_ref, decay_ref, seeds_ref, tiles_ref, out_ref, acc, blocks):
+def step_kernel(place_ref, row_ref, asked_ref, arrived_ref, decay_ref, seeds_ref, tiles_ref,
+                out_ref, acc, blocks):
     products(place_ref, row_ref, arrived_ref, tiles_ref, acc)
     update(asked_ref, decay_ref, seeds_ref, out_ref, acc, blocks)
 
@@ -154,33 +166,41 @@
 
     f32, i32 = jnp.float32, jnp.int32
     shape = jax.ShapeDtypeStruct
-    wanted, place, row, column, rounded = pl.pallas_call(
+    group = panels // 2
+    halves = [[h * group + g for g in range(group)] for h in range(2)]
+    across = [(p, (p + group) % panels) for p in range(panels)]
+    half = (lax.axis_index("row") // group).astype(i32).reshape(1)
+    wanted, near_place, place, row, column, rounded = pl.pallas_call(
         index_kernel,
-        out_shape=(shape((panels, 1, NEED), i32), shape((1, slots), i32), shape((1, slots), i32),
+        out_shape=(shape((panels, 1, 2 * NEED), i32), shape((1, slots), i32), shape((1, slots), i32), shape((1, slots), i32),
                    shape((seed_count, 1), f32), shape(blocks_shape, jnp.bfloat16)),
-        in_specs=[smem, hbm, hbm, hbm, hbm], out_specs=(vmem,) * 5,
+        in_specs=[smem, smem, hbm, hbm, hbm, hbm], out_specs=(vmem,) * 6,
         scratch_shapes=[pltpu.VMEM((1, slots), i32), pltpu.VMEM((1, slots), i32), pltpu.VMEM((1, seed_count), f32),
                         seeds_v, dma((4,))],
         compiler_params=small, name="index",
-    )(tile_count, in_hbm(tile_cols.reshape(1, slots)), in_hbm(tile_rows.reshape(1, slots)),
+    )(tile_count, half, in_hbm(tile_cols.reshape(1, slots)), in_hbm(tile_rows.reshape(1, slots)),
       in_hbm(decay.reshape(1, seed_count)), in_hbm(seeds))
-    asked = lax.all_to_all(wanted, "row", split_axis=0, concat_axis=0, tiled=True).reshape(panels, NEED)
+    other = lax.ppermute(rounded, "row", across)
+    asked = lax.all_to_all(wanted, "row", split_axis=0, concat_axis=0, tiled=True)
+    asked = asked.reshape(panels, 2 * NEED)
     outgoing = pl.pallas_call(
-        first_pack_kernel, out_shape=packed, in_specs=[smem, vmem], out_specs=vmem,
+        first_pack_kernel, out_shape=packed, in_specs=[smem, smem, vmem, vmem], out_specs=vmem,
         compiler_params=small, name="first_pack",
-        cost_estimate=pl.CostEstimate(flops=20_000_000_000, bytes_accessed=2 * mib, transcendentals=0))(asked, rounded)
+        cost_estimate=pl.CostEstimate(flops=20_000_000_000, bytes_accessed=2 * mib, transcendentals=0),
+    )(half, asked, rounded, other)
 
     for step in range(ITERS):
-        arrived = lax.all_to_all(outgoing, "row", split_axis=0, concat_axis=0, tiled=True)
+        arrived = lax.all_to_all(
+            outgoing, "row", split_axis=0, concat_axis=0, tiled=True, axis_index_groups=None if step else halves)
         if step == 0:
             outgoing, turned = pl.pallas_call(
                 turn_step_kernel, out_shape=(packed, shape(tiles.shape, tiles.dtype)),
-                in_specs=[smem, smem, smem, vmem, vmem, vmem, vmem], out_specs=(vmem, vmem),
+                in_specs=[smem] * 3 + [vmem] * 4, out_specs=(vmem, vmem),
                 scratch_shapes=[acc, blocks], compiler_params=small, name="turn_step",
-            )(place, row, asked, arrived, column, seeds, tiles)
+            )(near_place, row, asked, arrived, column, seeds, tiles)
         elif step < ITERS - 1:
             outgoing = pl.pallas_call(
-                step_kernel, out_shape=packed, in_specs=[smem, smem, smem, vmem, vmem, vmem, vmem], out_specs=vmem,
+                step_kernel, out_shape=packed, in_specs=[smem] * 3 + [vmem] * 4, out_specs=vmem,
                 scratch_shapes=[acc, blocks], compiler_params=small, name="step",
             )(place, row, asked, arrived, column, seeds, turned)
         else:

time: 99.4 us -> 97.9 us (0.985)
  blocking collectives: 87.5 us -> 82.1 us
  starting transfers between devices: 0 us -> 3.82 us
    ppermute x0 -> x1, starting transfers between devices: none -> 3.82 us  [per_device(): other = lax.ppermute(rounded, 'row', across)]
    all_to_all x1, blocking collectives: 15.2 us -> 12.1 us  [per_device(): lax.all_to_all(wanted, 'row', split_axis=0, concat_axis=0, tiled=True)]
    all_to_all x3, blocking collectives: 61.4 us -> 59.2 us  [per_device(): lax.all_to_all(outgoing, 'row', split_axis=0, concat_axis=0, tiled=True,...]
  transfers between devices with their start and end apart: 0 -> 1, of which waited for: 0 -> 0; matrix products, arithmetic and copies ran while one was open for 0% -> 0% of each run, Pallas kernels for 0% -> 0%
where the time goes in v3:
time: 97.9 us; the launch traced here: 97.6 us
  blocking collectives  82.1 us (84%)
  Pallas kernels  11 us (11%)
  starting transfers between devices  3.82 us (4%)
    all_to_all x3, blocking collectives, per_device(): lax.all_to_all(outgoing, 'row', split_axis=0, concat_axis=0, tiled=True,...  59.2 us
    all_to_all x1, blocking collectives, per_device(): lax.all_to_all(wanted, 'row', split_axis=0, concat_axis=0, tiled=True)  12.1 us
    all_to_all x1, blocking collectives, per_device(): lax.all_to_all(squares, 'row', split_axis=0, concat_axis=0, tiled=True)  10.9 us
    ppermute x1, starting transfers between devices, per_device(): other = lax.ppermute(rounded, 'row', across)  3.82 us
    pallas_call x1, Pallas kernels, per_device(): pl.pallas_call(turn_step_kernel, out_shape=(packed, shape(tiles.shape, ti...  3.43 us
    pallas_call x1, Pallas kernels, per_device(): pl.pallas_call(step_kernel, out_shape=packed, in_specs=[smem] * 3 + [vmem...  2.36 us
    pallas_call x1, Pallas kernels, per_device(): pl.pallas_call(last_kernel, out_shape=(shape(seeds.shape, f32), shape((pa...  2.32 us
  transfers between devices with their start and end apart: 1, of which 0 were waited for; matrix products, arithmetic and copies ran while one was open for 0% of the time, Pallas kernels for 0%

profile of v3, /device:TPU:1, one launch (start us, length us, event | category | flops | bytes accessed | tf_op | source)
XLA Modules:
  0.0 97.6 jit_solution(11005122857392833622)
XLA Ops:
  0.7 1.2 %index.1 = (s32[16,1,8]{2,1,0:T(1,128)S(1)}, s32[1,64]{1,0:T(1,128)S(1)}, s32[1,64]{1,0:T(1,128)S(1)}, s32[1,64]{1,0:T(1,128)S(1)}, f32[32,1]{1,0:T(8,128)S(1)}, /*index=5*/bf16[16,32,256]{2,1,0:T(8,128)(2,1)S(1)}) custom-call(s32[1]{0:T(128)S(6)} %copy.12.count_ref, s32[1]{0:T(128)} %bitcast.half_ref, s32[1,64]{1,0:T(1,128)} %bitcast.8, s32[1,64]{1,0:T(1,128)} %bitcast.9, ...), custom_call_target="tpu_custom_call" | custom-call | tf_op jit(solution)/shard_map/index/pallas_call | solution.py:173
  1.8 3.8 %collective-permute-start = (bf16[16,32,256]{2,1,0:T(8,128)(2,1)S(1)}, bf16[16,32,256]{2,1,0:T(8,128)(2,1)S(1)}, u32[]{:S(2)}, u32[]{:S(2)}) collective-permute-start(bf16[16,32,256]{2,1,0:T(8,128)(2,1)S(1)} %get-tuple-element.19.rounded_ref), channel_id=1, source_target_pairs={{0,8},{1,9},{2,10},{3,11},{4,12},{5,13},{6,14},{7,15},{8,0},{9,1},... | collective-permute-start | bytes 786440 | tf_op jit(solution)/shard_map/ppermute | solution.py:183
  5.6 12.1 %all_to_all.25 = s32[16,1,8]{2,1,0:T(1,128)S(1)} all-to-all(s32[16,1,8]{2,1,0:T(1,128)S(1)} %get-tuple-element.17), channel_id=1, replica_groups=mesh['graph'=16,'row'=16] {'row'}, dimensions={0} | all-to-all | bytes 1024 | tf_op jit(solution)/shard_map/all_to_all | solution.py:184
  17.7 0.0 collective-permute-done.other_ref
  17.7 0.0 copy-start
  17.7 0.0 copy-start.1
  17.7 0.7 first_pack.1
  18.5 18.4 %all_to_all.26.arrived_ref = bf16[64,32,256]{2,1,0:T(8,128)(2,1)S(1)} all-to-all(bf16[64,32,256]{2,1,0:T(8,128)(2,1)S(1)} %first_pack.1), channel_id=1, replica_groups={{0,1,2,3,4,5,6,7},{8,9,10,11,12,13,14,15},{16,17,18,19,20,21,22,23},{24..., dimensions={0} | all-to-all | bytes 2097152 | tf_op jit(solution)/shard_map/all_to_all | solution.py:193
  36.9 0.0 copy-done
  36.9 0.0 copy-done.1
  36.9 3.4 %turn_step.1 = (bf16[64,32,256]{2,1,0:T(8,128)(2,1)S(1)}, bf16[64,256,256]{2,1,0:T(8,128)(2,1)S(1)}) custom-call(s32[1,64]{1,0:T(1,128)S(1)} %get-tuple-element.18.place_ref, s32[1,64]{1,0:T(1,128)S(1)} %get-tuple-element.16.row_ref, s32[16,8]{1,0:T(8,128)S(1)} %bitcast.6, bf16[64,32,256]{2,1,0:T(8,128)(2,1)S(1)} %all_to_all.26.arrived_ref, ...), custom_call_target="tpu_custom_call" | custom-call | tf_op jit(solution)/shard_map/turn_step/pallas_call | solution.py:196
  40.3 20.2 %all_to_all.27.arrived_ref = bf16[64,32,256]{2,1,0:T(8,128)(2,1)S(1)} all-to-all(bf16[64,32,256]{2,1,0:T(8,128)(2,1)S(1)} %get-tuple-element.21), channel_id=1, replica_groups=mesh['graph'=16,'row'=16] {'row'}, dimensions={0} | all-to-all | bytes 2097152 | tf_op jit(solution)/shard_map/all_to_all | solution.py:193
  60.5 2.4 %step.1 = bf16[64,32,256]{2,1,0:T(8,128)(2,1)S(1)} custom-call(s32[1,64]{1,0:T(1,128)S(1)} %get-tuple-element.15.place_ref, s32[1,64]{1,0:T(1,128)S(1)} %get-tuple-element.16.row_ref, s32[16,8]{1,0:T(8,128)S(1)} %bitcast.7, bf16[64,32,256]{2,1,0:T(8,128)(2,1)S(1)} %all_to_all.27.arrived_ref, f32[32,1]{1,0:T(8,128)S(1)} %get-tuple-element.20.decay_ref, ...), custom_call_target="tpu_custom_call" | custom-call | tf_op jit(solution)/shard_map/step/pallas_call | solution.py:202
  62.9 20.6 %all_to_all.28.arrived_ref = bf16[64,32,256]{2,1,0:T(8,128)(2,1)S(1)} all-to-all(bf16[64,32,256]{2,1,0:T(8,128)(2,1)S(1)} %step.1), channel_id=1, replica_groups=mesh['graph'=16,'row'=16] {'row'}, dimensions={0} | all-to-all | bytes 2097152 | tf_op jit(solution)/shard_map/all_to_all | solution.py:193
  83.5 2.3 %last.1 = (f32[32,4096]{1,0:T(8,128)S(1)}, f32[16,1,32]{2,1,0:T(1,128)S(1)}) custom-call(s32[1,64]{1,0:T(1,128)S(1)} %get-tuple-element.15.place_ref, s32[1,64]{1,0:T(1,128)S(1)} %get-tuple-element.16.row_ref, bf16[64,32,256]{2,1,0:T(8,128)(2,1)S(1)} %all_to_all.28.arrived_ref, f32[32,1]{1,0:T(8,128)S(1)} %get-tuple-element.20.decay_ref, ...), custom_call_target="tpu_custom_call" | custom-call | tf_op jit(solution)/shard_map/last/pallas_call | solution.py:207
  85.8 10.9 %all_to_all.29.squares_ref = f32[16,1,32]{2,1,0:T(1,128)S(1)} all-to-all(f32[16,1,32]{2,1,0:T(1,128)S(1)} %get-tuple-element.23), channel_id=1, replica_groups=mesh['graph'=16,'row'=16] {'row'}, dimensions={0} | all-to-all | bytes 4096 | tf_op jit(solution)/shard_map/all_to_all | solution.py:212
  96.7 0.9 scale.1
Async XLA Ops:
  1.8 15.9 %collective-permute-start = (bf16[16,32,256]{2,1,0:T(8,128)(2,1)S(1)}, bf16[16,32,256]{2,1,0:T(8,128)(2,1)S(1)}, u32[]{:S(2)}, u32[]{:S(2)}) collective-permute-start(bf16[16,32,256]{2,1,0:T(8,128)(2,1)S(1)} %get-tuple-element.19.rounded_ref), channel_id=1, source_target_pairs={{0,8},{1,9},{2,10},{3,11},{4,12},{5,13},{6,14},{7,15},{8,0},{9,1},... | collective-permute-start | bytes 786440 | tf_op jit(solution)/shard_map/ppermute | solution.py:183
  17.7 19.2 %copy-start = (f32[32,4096]{1,0:T(8,128)S(1)}, f32[32,4096]{1,0:T(8,128)}, u32[]{:S(2)}) copy-start(f32[32,4096]{1,0:T(8,128)} %seeds_ref.7) | copy-start | bytes 1572868
  17.7 19.2 %copy-start.1 = (bf16[64,256,256]{2,1,0:T(8,128)(2,1)S(1)}, bf16[64,256,256]{2,1,0:T(8,128)(2,1)}, u32[]{:S(2)}) copy-start(bf16[64,256,256]{2,1,0:T(8,128)(2,1)} %tiles_ref.1) | copy-start | bytes 25165828

commit v4 on v2

--- a/solution.py
+++ b/solution.py
@@ -1,5 +1,3 @@
-import functools
-
 import jax
 import jax.numpy as jnp
 from jax import lax
@@ -7,19 +5,23 @@
 from jax.experimental.pallas import tpu as pltpu
 from jax.sharding import PartitionSpec as P
 
+
 TILE = 256
 NEED = 4
 ITERS = 3
+TURN = 4
+ORDER = (4, 2, 6)
 
 
 def in_hbm(x):
     return pltpu.with_memory_space_constraint(x, pltpu.HBM)
 
 
-def index_kernel(count_ref, cols_ref, rows_ref, decay_ref, seeds_ref, wanted_ref, place_ref, row_ref, column_ref,
+def index_kernel(count_ref, own_ref, cols_ref, rows_ref, decay_ref, seeds_ref, wanted_ref, near_place_ref, place_ref, row_ref, column_ref,
                  rounded_ref, cols_v, rows_v, decay_v, seeds_v, sems):
     blk = rounded_ref.shape[0]
-    panels = wanted_ref.shape[0]
+    group = wanted_ref.shape[0]
+    panels = 2 * group
     slots = cols_v.shape[1]
     seed_count = seeds_v.shape[0]
     gets = []
@@ -41,14 +43,23 @@
         for k in range(NEED):
             picks[k] = jnp.where((here > 0) & (rank == k), float(b), picks[k])
         rank = rank + here
-    lane = lax.broadcasted_iota(jnp.int32, (panels, NEED), 1)
-    wanted = jnp.zeros((panels, NEED), jnp.float32)
+    half = own_ref[0] // group
+    own = own_ref[0] % group
+    lane = lax.broadcasted_iota(jnp.int32, (group, 2 * NEED), 1)
+    wanted = jnp.zeros((group, 2 * NEED), jnp.float32)
     for k in range(NEED):
-        wanted = jnp.where(lane == k, picks[k], wanted)
+        near = jnp.where(half == 0, picks[k][:group], picks[k][group:])
+        far = jnp.where(half == 0, picks[k][group:], picks[k][:group])
+        wanted = jnp.where(lane == k, near, jnp.where(lane == NEED + k, far, wanted))
     wanted = wanted.astype(jnp.int32)
-    for q in range(panels):
-        wanted_ref[q] = wanted[q:q + 1]
+    for g in range(group):
+        wanted_ref[g] = wanted[g:g + 1]
     place_ref[...] = jnp.sum(spot, axis=0, keepdims=True).astype(jnp.int32)
+    side = jnp.where((panel >= group) == (half == 1), 0, NEED)
+    away = (panel % group) ^ own
+    shift = (away * 2 * NEED + side - panel * NEED).astype(jnp.float32)
+    near_spot = jnp.where(local >= 0, jnp.where(local < blk, spot + shift, 0.0), 0.0)
+    near_place_ref[...] = jnp.sum(near_spot, axis=0, keepdims=True).astype(jnp.int32)
     gets[1].wait()
     row_ref[...] = jnp.where(live[:1], rows_v[...], blk)
     gets[2].wait()
@@ -64,44 +75,70 @@
     return jnp.sum(jnp.where(diagonal, jnp.broadcast_to(x, square), 0.0), axis=1, keepdims=True)
 
 
-def send_blocks(blocks, asked_ref, out_ref):
-    for slot in range(out_ref.shape[0]):
-        out_ref[slot] = blocks[asked_ref[slot // NEED, slot % NEED]]
-
-
-def first_pack_kernel(asked_ref, rounded_ref, out_ref):
-    send_blocks(rounded_ref, asked_ref, out_ref)
-
-
-def products(place_ref, row_ref, arrived_ref, tiles_ref, acc, turned_ref=None):
+def first_pack_kernel(own_ref, asked_ref, rounded_ref, other_ref, *out_refs):
+    for r in range(asked_ref.shape[0]):
+        out_ref, at = (out_refs[r], 0) if r < 2 else (out_refs[r // 2 + 1], r % 2 * 2 * NEED)
+        g = (own_ref[0] % asked_ref.shape[0]) ^ r
+        for k in range(NEED):
+            out_ref[at + k] = rounded_ref[asked_ref[g, k]]
+            out_ref[at + NEED + k] = other_ref[asked_ref[g, NEED + k]]
+
+
+def turn_kernel(tiles_ref, out_ref, buf, sems):
+    chunk = buf.shape[0] // sems.shape[0]
+    parts = [pl.ds(c * chunk, chunk) for c in range(sems.shape[0])]
+    gets = [pltpu.make_async_copy(tiles_ref.at[p], buf.at[p], sems.at[c]) for c, p in enumerate(parts)]
+    for get in gets:
+        get.start()
+    for c, get in enumerate(gets):
+        get.wait()
+
+        def body(i, carry, c=c):
+            for k in range(TURN):
+                t = c * chunk + i * TURN + k
+                out_ref[t] = buf[t].T
+            return carry
+
+        lax.fori_loop(0, chunk // TURN, body, 0)
+
+
+def send_blocks(blocks, own_ref, asked_ref, far_ref, out_ref):
+    group = asked_ref.shape[0]
+    near = own_ref[0] // group * group
+    for g in range(group):
+        for k in range(NEED):
+            out_ref[(near + g) * NEED + k] = blocks[asked_ref[g, k]]
+            out_ref[(group - near + g) * NEED + k] = blocks[far_ref[g, NEED + k]]
+
+
+def products(place_ref, row_ref, arrived_ref, tiles_ref, acc):
     acc[...] = jnp.zeros(acc.shape, acc.dtype)
     for t in range(tiles_ref.shape[0]):
         x = arrived_ref[place_ref[0, t]]
-        if turned_ref is None:
-            y = jnp.dot(x, tiles_ref[t], preferred_element_type=jnp.float32)
-        else:
-            tile = tiles_ref[t]
-            turned_ref[t] = tile.T
-            y = lax.dot_general(x, tile, (((1,), (1,)), ((), ())), preferred_element_type=jnp.float32)
-        acc[row_ref[0, t]] += y
-
-
-def update(asked_ref, decay_ref, seeds_ref, out_ref, acc, blocks):
+        acc[row_ref[0, t]] += jnp.dot(x, tiles_ref[t], preferred_element_type=jnp.float32)
+
+
+def update(own_ref, asked_ref, far_ref, decay_ref, seeds_ref, out_ref, acc, blocks):
     decay = decay_ref[...]
     for b in range(blocks.shape[0]):
         blocks[b] = (decay * acc[b] + seeds_ref[:, b * TILE:(b + 1) * TILE]).astype(jnp.bfloat16)
-    send_blocks(blocks, asked_ref, out_ref)
-
-
-def turn_step_kernel(place_ref, row_ref, asked_ref, arrived_ref, decay_ref, seeds_ref, tiles_ref,
-                     out_ref, turned_ref, acc, blocks):
-    products(place_ref, row_ref, arrived_ref, tiles_ref, acc, turned_ref)
-    update(asked_ref, decay_ref, seeds_ref, out_ref, acc, blocks)
-
-
-def step_kernel(place_ref, row_ref, asked_ref, arrived_ref, decay_ref, seeds_ref, tiles_ref, out_ref, acc, blocks):
+    send_blocks(blocks, own_ref, asked_ref, far_ref, out_ref)
+
+
+def first_step_kernel(place_ref, row_ref, own_ref, asked_ref, far_ref, *refs):
+    arrived_refs, (decay_ref, seeds_ref, tiles_ref, out_ref, arrived, acc, blocks) = refs[:-7], refs[-7:]
+    each = 2 * NEED
+    for r in range(arrived.shape[0] // each):
+        ref, at = (arrived_refs[r], 0) if r < 2 else (arrived_refs[r], r % 2 * each)
+        arrived[r * each:(r + 1) * each] = ref[at:at + each]
+    products(place_ref, row_ref, arrived, tiles_ref, acc)
+    update(own_ref, asked_ref, far_ref, decay_ref, seeds_ref, out_ref, acc, blocks)
+
+
+def step_kernel(place_ref, row_ref, own_ref, asked_ref, far_ref, arrived_ref, decay_ref, seeds_ref, tiles_ref,
+                out_ref, acc, blocks):
     products(place_ref, row_ref, arrived_ref, tiles_ref, acc)
-    update(asked_ref, decay_ref, seeds_ref, out_ref, acc, blocks)
+    update(own_ref, asked_ref, far_ref, decay_ref, seeds_ref, out_ref, acc, blocks)
 
 
 def last_kernel(place_ref, row_ref, arrived_ref, decay_ref, seeds_ref, tiles_ref, out_ref, squares_ref, acc):
@@ -154,35 +191,60 @@
 
     f32, i32 = jnp.float32, jnp.int32
     shape = jax.ShapeDtypeStruct
-    wanted, place, row, column, rounded = pl.pallas_call(
+    group = panels // 2
+    halves = [[h * group + g for g in range(group)] for h in range(2)]
+    own = lax.axis_index("row").astype(i32).reshape(1)
+
+    def away(x, r):
+        return lax.ppermute(x, "row", [(p, p ^ r) for p in range(panels)])
+
+    wanted, near_place, place, row, column, rounded = pl.pallas_call(
         index_kernel,
-        out_shape=(shape((panels, 1, NEED), i32), shape((1, slots), i32), shape((1, slots), i32),
+        out_shape=(shape((group, 1, 2 * NEED), i32), shape((1, slots), i32), shape((1, slots), i32), shape((1, slots), i32),
                    shape((seed_count, 1), f32), shape(blocks_shape, jnp.bfloat16)),
-        in_specs=[smem, hbm, hbm, hbm, hbm], out_specs=(vmem,) * 5,
+        in_specs=[smem, smem, hbm, hbm, hbm, hbm], out_specs=(vmem,) * 6,
         scratch_shapes=[pltpu.VMEM((1, slots), i32), pltpu.VMEM((1, slots), i32), pltpu.VMEM((1, seed_count), f32),
                         seeds_v, dma((4,))],
         compiler_params=small, name="index",
-    )(tile_count, in_hbm(tile_cols.reshape(1, slots)), in_hbm(tile_rows.reshape(1, slots)),
+    )(tile_count, own, in_hbm(tile_cols.reshape(1, slots)), in_hbm(tile_rows.reshape(1, slots)),
       in_hbm(decay.reshape(1, seed_count)), in_hbm(seeds))
-    asked = lax.all_to_all(wanted, "row", split_axis=0, concat_axis=0, tiled=True).reshape(panels, NEED)
+    other = away(rounded, group)
+    asked = lax.all_to_all(wanted, "row", split_axis=0, concat_axis=0, tiled=True, axis_index_groups=halves)
+    asked = asked.reshape(group, 2 * NEED)
+    chip = shape((2 * NEED, seed_count, TILE), jnp.bfloat16)
+    pair = shape((4 * NEED, seed_count, TILE), jnp.bfloat16)
+    chips = group // 2
+    sent = pl.pallas_call(
+        first_pack_kernel, out_shape=(chip, chip) + (pair,) * (chips - 1),
+        in_specs=[smem, smem, vmem, vmem], out_specs=(vmem,) * (chips + 1),
+        compiler_params=small, name="first_pack",
+    )(own, asked, rounded, other)
+    tiles, *sent = lax.optimization_barrier((tiles, *sent))
+    turned = pl.pallas_call(
+        turn_kernel, out_shape=shape(tiles.shape, tiles.dtype), in_specs=[hbm], out_specs=vmem,
+        scratch_shapes=[pltpu.VMEM(tiles.shape, tiles.dtype), dma((8,))],
+        compiler_params=pltpu.CompilerParams(vmem_limit_bytes=12 * mib), name="turn_tiles",
+        cost_estimate=pl.CostEstimate(flops=6_000_000_000, bytes_accessed=8 * mib, transcendentals=0),
+    )(in_hbm(tiles))
+    direct = []
+    for r in ORDER:
+        direct.append(away(sent[r // 2 + 1], r))
+    far = away(asked, group)
+    arrived = {0: sent[0], 1: away(sent[1], 1)}
+    for r, x in zip(ORDER, direct):
+        arrived[r] = x
+        arrived[r + 1] = away(x, 1)
     outgoing = pl.pallas_call(
-        first_pack_kernel, out_shape=packed, in_specs=[smem, vmem], out_specs=vmem,
-        compiler_params=small, name="first_pack",
-        cost_estimate=pl.CostEstimate(flops=20_000_000_000, bytes_accessed=2 * mib, transcendentals=0))(asked, rounded)
-
-    for step in range(ITERS):
+        first_step_kernel, out_shape=packed, in_specs=[smem] * 5 + [vmem] * (group + 3), out_specs=vmem,
+        scratch_shapes=[pltpu.VMEM(packed.shape, packed.dtype), acc, blocks], compiler_params=small, name="first_step",
+    )(near_place, row, own, asked, far, *[arrived[r] for r in range(group)], column, seeds, turned)
+    for step in range(1, ITERS):
         arrived = lax.all_to_all(outgoing, "row", split_axis=0, concat_axis=0, tiled=True)
-        if step == 0:
-            outgoing, turned = pl.pallas_call(
-                turn_step_kernel, out_shape=(packed, shape(tiles.shape, tiles.dtype)),
-                in_specs=[smem, smem, smem, vmem, vmem, vmem, vmem], out_specs=(vmem, vmem),
-                scratch_shapes=[acc, blocks], compiler_params=small, name="turn_step",
-            )(place, row, asked, arrived, column, seeds, tiles)
-        elif step < ITERS - 1:
+        if step < ITERS - 1:
             outgoing = pl.pallas_call(
-                step_kernel, out_shape=packed, in_specs=[smem, smem, smem, vmem, vmem, vmem, vmem], out_specs=vmem,
+                step_kernel, out_shape=packed, in_specs=[smem] * 5 + [vmem] * 4, out_specs=vmem,
                 scratch_shapes=[acc, blocks], compiler_params=small, name="step",
-            )(place, row, asked, arrived, column, seeds, turned)
+            )(place, row, own, asked, far, arrived, column, seeds, turned)
         else:
             iterate, squares = pl.pallas_call(
                 last_kernel, out_shape=(shape(seeds.shape, f32), shape((panels, 1, seed_count), f32)),
@@ -204,5 +266,6 @@
         P(None, ("graph", "row")),
         P(),
     )
+
     return jax.shard_map(
         per_device, mesh=mesh, in_specs=in_specs, out_specs=P(None, ("graph", "row")), check_vma=False)

time: 99.4 us -> 97.8 us (0.984)
  blocking collectives: 87.5 us -> 61 us
  starting transfers between devices: 0 us -> 16.1 us
  waiting for transfers between devices: 0 us -> 5.48 us
  Pallas kernels: 10.9 us -> 14.3 us
    all_to_all x3 -> x2, blocking collectives: 61.4 us -> 40.5 us  [per_device(): lax.all_to_all(outgoing, 'row', split_axis=0, concat_axis=0, tiled=True)]
    ppermute x0 -> x9, starting transfers between devices: none -> 16.1 us  [away(): return lax.ppermute(x, 'row', [(p, p ^ r) for p in range(panels)])]
    all_to_all x1, blocking collectives: 15.2 us -> 9.64 us  [per_device(): lax.all_to_all(wanted, 'row', split_axis=0, concat_axis=0, tiled=True, ax...]
    ppermute x0 -> x9, waiting for transfers between devices: none -> 5.48 us  [away(): return lax.ppermute(x, 'row', [(p, p ^ r) for p in range(panels)])]
    pallas_call x4 -> x5, Pallas kernels: 7.67 us -> 11 us  [the longest x1 4.34 us: per_device(): pl.pallas_call(turn_kernel, out_shape=shape(tiles.shape, tiles.dtype), in...]
  transfers between devices with their start and end apart: 0 -> 9, of which waited for: 0 -> 3; matrix products, arithmetic and copies ran while one was open for 0% -> 0% of each run, Pallas kernels for 0% -> 4%
where the time goes in v4:
time: 97.8 us; the launch traced here: 97.6 us
  blocking collectives  61 us (62%)
  starting transfers between devices  16.1 us (16%)
  Pallas kernels  14.3 us (15%)
  waiting for transfers between devices  5.48 us (6%)
    all_to_all x2, blocking collectives, per_device(): lax.all_to_all(outgoing, 'row', split_axis=0, concat_axis=0, tiled=True)  40.5 us
    ppermute x9, starting transfers between devices, away(): return lax.ppermute(x, 'row', [(p, p ^ r) for p in range(panels)])  16.1 us
    all_to_all x1, blocking collectives, per_device(): lax.all_to_all(squares, 'row', split_axis=0, concat_axis=0, tiled=True)  10.9 us
    all_to_all x1, blocking collectives, per_device(): lax.all_to_all(wanted, 'row', split_axis=0, concat_axis=0, tiled=True, ax...  9.64 us
    ppermute x9, waiting for transfers between devices, away(): return lax.ppermute(x, 'row', [(p, p ^ r) for p in range(panels)])  5.48 us
    pallas_call x1, Pallas kernels, per_device(): pl.pallas_call(turn_kernel, out_shape=shape(tiles.shape, tiles.dtype), in...  4.34 us
    pallas_call x1, Pallas kernels, per_device(): pl.pallas_call(first_step_kernel, out_shape=packed, in_specs=[smem] * 5 +...  2.45 us
    pallas_call x1, Pallas kernels, per_device(): pl.pallas_call(step_kernel, out_shape=packed, in_specs=[smem] * 5 + [vmem...  2.38 us
  transfers between devices with their start and end apart: 9, of which 3 were waited for; matrix products, arithmetic and copies ran while one was open for 0% of the time, Pallas kernels for 4%

profile of v4, /device:TPU:1, one launch (start us, length us, event | category | flops | bytes accessed | tf_op | source)
XLA Modules:
  0.0 97.6 jit_solution(5587486370388322451)
XLA Ops:
  0.7 1.2 %index.1 = (s32[8,1,8]{2,1,0:T(1,128)S(1)}, s32[1,64]{1,0:T(1,128)S(1)}, s32[1,64]{1,0:T(1,128)S(1)}, s32[1,64]{1,0:T(1,128)S(1)}, f32[32,1]{1,0:T(8,128)S(1)}, /*index=5*/bf16[16,32,256]{2,1,0:T(8,128)(2,1)S(1)}) custom-call(s32[1]{0:T(128)S(6)} %copy.7.count_ref, s32[1]{0:T(128)} %bitcast.own_ref, s32[1,64]{1,0:T(1,128)} %bitcast.9, s32[1,64]{1,0:T(1,128)} %bitcast.10, ...), custom_call_target="tpu_custom_call" | custom-call | tf_op jit(solution)/shard_map/index/pallas_call | solution.py:201
  1.8 3.8 %collective-permute-start.1 = (bf16[16,32,256]{2,1,0:T(8,128)(2,1)S(1)}, bf16[16,32,256]{2,1,0:T(8,128)(2,1)S(1)}, u32[]{:S(2)}, u32[]{:S(2)}) collective-permute-start(bf16[16,32,256]{2,1,0:T(8,128)(2,1)S(1)} %get-tuple-element.28.rounded_ref), channel_id=1, source_target_pairs={{0,8},{1,9},{2,10},{3,11},{4,12},{5,13},{6,14},{7,15},{8,0},{9,1},... | collective-permute-start | bytes 786440 | tf_op jit(solution)/shard_map/ppermute | solution.py:199
  5.6 9.6 %all_to_all.20 = s32[8,1,8]{2,1,0:T(1,128)S(1)} all-to-all(s32[8,1,8]{2,1,0:T(1,128)S(1)} %get-tuple-element.26), channel_id=1, replica_groups={{0,1,2,3,4,5,6,7},{8,9,10,11,12,13,14,15},{16,17,18,19,20,21,22,23},{24..., dimensions={0} | all-to-all | bytes 512 | tf_op jit(solution)/shard_map/all_to_all | solution.py:212
  15.3 0.0 collective-permute-done.1.other_ref
  15.3 0.7 first_pack.1
  16.0 0.0 copy-start
  16.0 0.4 collective-permute-start.3
  16.3 1.8 %collective-permute-start.5 = (bf16[16,32,256]{2,1,0:T(8,128)(2,1)S(1)}, bf16[16,32,256]{2,1,0:T(8,128)(2,1)S(1)}, u32[]{:S(2)}, u32[]{:S(2)}) collective-permute-start(bf16[16,32,256]{2,1,0:T(8,128)(2,1)S(1)} %get-tuple-element.37), channel_id=1, source_target_pairs={{0,4},{1,5},{2,6},{3,7},{4,0},{5,1},{6,2},{7,3},{8,12},{9,13},{10,... | collective-permute-start | bytes 786440 | tf_op jit(solution)/shard_map/ppermute | solution.py:199
  18.1 1.8 %collective-permute-start.7 = (bf16[16,32,256]{2,1,0:T(8,128)(2,1)S(1)}, bf16[16,32,256]{2,1,0:T(8,128)(2,1)S(1)}, u32[]{:S(2)}, u32[]{:S(2)}) collective-permute-start(bf16[16,32,256]{2,1,0:T(8,128)(2,1)S(1)} %get-tuple-element.38), channel_id=1, source_target_pairs={{0,6},{1,7},{2,4},{3,5},{4,2},{5,3},{6,0},{7,1},{8,14},{9,15},{10,... | collective-permute-start | bytes 786440 | tf_op jit(solution)/shard_map/ppermute | solution.py:199
  19.9 0.1 collective-permute-start
  20.0 1.8 %collective-permute-start.2 = (bf16[8,32,256]{2,1,0:T(8,128)(2,1)S(1)}, bf16[8,32,256]{2,1,0:T(8,128)(2,1)S(1)}, u32[]{:S(2)}, u32[]{:S(2)}) collective-permute-start(bf16[8,32,256]{2,1,0:T(8,128)(2,1)S(1)} %get-tuple-element.35), channel_id=1, source_target_pairs={{0,1},{1,0},{2,3},{3,2},{4,5},{5,4},{6,7},{7,6},{8,9},{9,8},{10,11... | collective-permute-start | bytes 393224 | tf_op jit(solution)/shard_map/ppermute | solution.py:199
  21.8 1.4 %collective-permute-done.3.refs_2_ = bf16[16,32,256]{2,1,0:T(8,128)(2,1)S(1)} collective-permute-done((bf16[16,32,256]{2,1,0:T(8,128)(2,1)S(1)}, bf16[16,32,256]{2,1,0:T(8,128)(2,1)S(1)}, u32[]{:S(2)}, u32[]{:S(2)}) %collective-permute-start.3) | collective-permute-done | bytes 262176 | tf_op jit(solution)/shard_map/ppermute | solution.py:199
  23.2 2.7 %collective-permute-start.4 = (bf16[16,32,256]{2,1,0:T(8,128)(2,1)S(1)}, bf16[16,32,256]{2,1,0:T(8,128)(2,1)S(1)}, u32[]{:S(2)}, u32[]{:S(2)}) collective-permute-start(bf16[16,32,256]{2,1,0:T(8,128)(2,1)S(1)} %collective-permute-done.3.refs_2_), channel_id=1, source_target_pairs={{0,1},{1,0},{2,3},{3,2},{4,5},{5,4},{6,7},{7,6},{8,9},{9,8},{10,11... | collective-permute-start | bytes 786440 | tf_op jit(solution)/shard_map/ppermute | solution.py:199
  25.9 3.6 %collective-permute-done.5.refs_4_ = bf16[16,32,256]{2,1,0:T(8,128)(2,1)S(1)} collective-permute-done((bf16[16,32,256]{2,1,0:T(8,128)(2,1)S(1)}, bf16[16,32,256]{2,1,0:T(8,128)(2,1)S(1)}, u32[]{:S(2)}, u32[]{:S(2)}) %collective-permute-start.5) | collective-permute-done | bytes 262176 | tf_op jit(solution)/shard_map/ppermute | solution.py:199
  29.5 1.6 %collective-permute-start.6 = (bf16[16,32,256]{2,1,0:T(8,128)(2,1)S(1)}, bf16[16,32,256]{2,1,0:T(8,128)(2,1)S(1)}, u32[]{:S(2)}, u32[]{:S(2)}) collective-permute-start(bf16[16,32,256]{2,1,0:T(8,128)(2,1)S(1)} %collective-permute-done.5.refs_4_), channel_id=1, source_target_pairs={{0,1},{1,0},{2,3},{3,2},{4,5},{5,4},{6,7},{7,6},{8,9},{9,8},{10,11... | collective-permute-start | bytes 786440 | tf_op jit(solution)/shard_map/ppermute | solution.py:199
  31.1 0.5 collective-permute-done.7.refs_6_
  31.6 2.1 %collective-permute-start.8 = (bf16[16,32,256]{2,1,0:T(8,128)(2,1)S(1)}, bf16[16,32,256]{2,1,0:T(8,128)(2,1)S(1)}, u32[]{:S(2)}, u32[]{:S(2)}) collective-permute-start(bf16[16,32,256]{2,1,0:T(8,128)(2,1)S(1)} %collective-permute-done.7.refs_6_), channel_id=1, source_target_pairs={{0,1},{1,0},{2,3},{3,2},{4,5},{5,4},{6,7},{7,6},{8,9},{9,8},{10,11... | collective-permute-start | bytes 786440 | tf_op jit(solution)/shard_map/ppermute | solution.py:199
  33.7 4.3 %turn_tiles.1.refs_10_.tiles_ref = bf16[64,256,256]{2,1,0:T(8,128)(2,1)S(1)} custom-call(bf16[64,256,256]{2,1,0:T(8,128)(2,1)} %tiles_ref), custom_call_target="tpu_custom_call" | custom-call | flops 6000000000 | bytes 8388608 | tf_op jit(solution)/shard_map/turn_tiles/pallas_call | solution.py:223
  38.0 0.0 collective-permute-done.far_ref
  38.0 0.0 collective-permute-done.2.refs_1_
  38.1 0.0 collective-permute-done.4.refs_3_
  38.1 0.0 collective-permute-done.6.refs_5_
  38.1 0.0 collective-permute-done.8.refs_7_
  38.1 0.0 copy-done
  38.1 2.5 %first_step.1 = bf16[64,32,256]{2,1,0:T(8,128)(2,1)S(1)} custom-call(s32[1,64]{1,0:T(1,128)S(1)} %get-tuple-element.27.place_ref, s32[1,64]{1,0:T(1,128)S(1)} %get-tuple-element.25.row_ref, s32[1]{0:T(128)} %bitcast.own_ref, s32[8,8]{1,0:T(8,128)S(1)} %bitcast.7, s32[8,8]{1,0:T(8,128)S(1)} %collective-permute-done.far_ref, ...), custom_call_target="tpu_custom_call" | custom-call | tf_op jit(solution)/shard_map/first_step/pallas_call | solution.py:237
  40.6 19.9 %all_to_all.21.arrived_ref = bf16[64,32,256]{2,1,0:T(8,128)(2,1)S(1)} all-to-all(bf16[64,32,256]{2,1,0:T(8,128)(2,1)S(1)} %first_step.1), channel_id=1, replica_groups=mesh['graph'=16,'row'=16] {'row'}, dimensions={0} | all-to-all | bytes 2097152 | tf_op jit(solution)/shard_map/all_to_all | solution.py:242
  60.4 2.4 %step.1 = bf16[64,32,256]{2,1,0:T(8,128)(2,1)S(1)} custom-call(s32[1,64]{1,0:T(1,128)S(1)} %get-tuple-element.24.place_ref, s32[1,64]{1,0:T(1,128)S(1)} %get-tuple-element.25.row_ref, s32[1]{0:T(128)} %bitcast.own_ref, s32[8,8]{1,0:T(8,128)S(1)} %bitcast.8, s32[8,8]{1,0:T(8,128)S(1)} %collective-permute-done.far_ref, ...), custom_call_target="tpu_custom_call" | custom-call | tf_op jit(solution)/shard_map/step/pallas_call | solution.py:244
  62.8 20.6 %all_to_all.22.arrived_ref = bf16[64,32,256]{2,1,0:T(8,128)(2,1)S(1)} all-to-all(bf16[64,32,256]{2,1,0:T(8,128)(2,1)S(1)} %step.1), channel_id=1, replica_groups=mesh['graph'=16,'row'=16] {'row'}, dimensions={0} | all-to-all | bytes 2097152 | tf_op jit(solution)/shard_map/all_to_all | solution.py:242
  83.4 2.3 %last.1 = (f32[32,4096]{1,0:T(8,128)S(1)}, f32[16,1,32]{2,1,0:T(1,128)S(1)}) custom-call(s32[1,64]{1,0:T(1,128)S(1)} %get-tuple-element.24.place_ref, s32[1,64]{1,0:T(1,128)S(1)} %get-tuple-element.25.row_ref, bf16[64,32,256]{2,1,0:T(8,128)(2,1)S(1)} %all_to_all.22.arrived_ref, f32[32,1]{1,0:T(8,128)S(1)} %get-tuple-element.39.refs_8_.decay_ref, ...), custom_call_target="tpu_custom_call" | custom-call | tf_op jit(solution)/shard_map/last/pallas_call | solution.py:249
  85.7 10.9 %all_to_all.23.squares_ref = f32[16,1,32]{2,1,0:T(1,128)S(1)} all-to-all(f32[16,1,32]{2,1,0:T(1,128)S(1)} %get-tuple-element.41), channel_id=1, replica_groups=mesh['graph'=16,'row'=16] {'row'}, dimensions={0} | all-to-all | bytes 4096 | tf_op jit(solution)/shard_map/all_to_all | solution.py:254
  96.6 0.9 scale.1
Async XLA Ops:
  1.8 13.5 %collective-permute-start.1 = (bf16[16,32,256]{2,1,0:T(8,128)(2,1)S(1)}, bf16[16,32,256]{2,1,0:T(8,128)(2,1)S(1)}, u32[]{:S(2)}, u32[]{:S(2)}) collective-permute-start(bf16[16,32,256]{2,1,0:T(8,128)(2,1)S(1)} %get-tuple-element.28.rounded_ref), channel_id=1, source_target_pairs={{0,8},{1,9},{2,10},{3,11},{4,12},{5,13},{6,14},{7,15},{8,0},{9,1},... | collective-permute-start | bytes 786440 | tf_op jit(solution)/shard_map/ppermute | solution.py:199
  16.0 22.1 %copy-start = (f32[32,4096]{1,0:T(8,128)S(1)}, f32[32,4096]{1,0:T(8,128)}, u32[]{:S(2)}) copy-start(f32[32,4096]{1,0:T(8,128)} %seeds_ref.5) | copy-start | bytes 1572868
  16.0 7.3 %collective-permute-start.3 = (bf16[16,32,256]{2,1,0:T(8,128)(2,1)S(1)}, bf16[16,32,256]{2,1,0:T(8,128)(2,1)S(1)}, u32[]{:S(2)}, u32[]{:S(2)}) collective-permute-start(bf16[16,32,256]{2,1,0:T(8,128)(2,1)S(1)} %get-tuple-element.36), channel_id=1, source_target_pairs={{0,2},{1,3},{2,0},{3,1},{4,6},{5,7},{6,4},{7,5},{8,10},{9,11},{10,... | collective-permute-start | bytes 786440 | tf_op jit(solution)/shard_map/ppermute | solution.py:199
  16.3 13.1 %collective-permute-start.5 = (bf16[16,32,256]{2,1,0:T(8,128)(2,1)S(1)}, bf16[16,32,256]{2,1,0:T(8,128)(2,1)S(1)}, u32[]{:S(2)}, u32[]{:S(2)}) collective-permute-start(bf16[16,32,256]{2,1,0:T(8,128)(2,1)S(1)} %get-tuple-element.37), channel_id=1, source_target_pairs={{0,4},{1,5},{2,6},{3,7},{4,0},{5,1},{6,2},{7,3},{8,12},{9,13},{10,... | collective-permute-start | bytes 786440 | tf_op jit(solution)/shard_map/ppermute | solution.py:199
  18.1 13.4 %collective-permute-start.7 = (bf16[16,32,256]{2,1,0:T(8,128)(2,1)S(1)}, bf16[16,32,256]{2,1,0:T(8,128)(2,1)S(1)}, u32[]{:S(2)}, u32[]{:S(2)}) collective-permute-start(bf16[16,32,256]{2,1,0:T(8,128)(2,1)S(1)} %get-tuple-element.38), channel_id=1, source_target_pairs={{0,6},{1,7},{2,4},{3,5},{4,2},{5,3},{6,0},{7,1},{8,14},{9,15},{10,... | collective-permute-start | bytes 786440 | tf_op jit(solution)/shard_map/ppermute | solution.py:199
  19.9 18.1 %collective-permute-start = (s32[8,8]{1,0:T(8,128)S(1)}, s32[8,8]{1,0:T(8,128)S(1)}, u32[]{:S(2)}, u32[]{:S(2)}) collective-permute-start(s32[8,8]{1,0:T(8,128)S(1)} %bitcast.6), channel_id=1, source_target_pairs={{0,8},{1,9},{2,10},{3,11},{4,12},{5,13},{6,14},{7,15},{8,0},{9,1},... | collective-permute-start | bytes 776 | tf_op jit(solution)/shard_map/ppermute | solution.py:199
  20.0 18.1 %collective-permute-start.2 = (bf16[8,32,256]{2,1,0:T(8,128)(2,1)S(1)}, bf16[8,32,256]{2,1,0:T(8,128)(2,1)S(1)}, u32[]{:S(2)}, u32[]{:S(2)}) collective-permute-start(bf16[8,32,256]{2,1,0:T(8,128)(2,1)S(1)} %get-tuple-element.35), channel_id=1, source_target_pairs={{0,1},{1,0},{2,3},{3,2},{4,5},{5,4},{6,7},{7,6},{8,9},{9,8},{10,11... | collective-permute-start | bytes 393224 | tf_op jit(solution)/shard_map/ppermute | solution.py:199
  23.2 14.8 %collective-permute-start.4 = (bf16[16,32,256]{2,1,0:T(8,128)(2,1)S(1)}, bf16[16,32,256]{2,1,0:T(8,128)(2,1)S(1)}, u32[]{:S(2)}, u32[]{:S(2)}) collective-permute-start(bf16[16,32,256]{2,1,0:T(8,128)(2,1)S(1)} %collective-permute-done.3.refs_2_), channel_id=1, source_target_pairs={{0,1},{1,0},{2,3},{3,2},{4,5},{5,4},{6,7},{7,6},{8,9},{9,8},{10,11... | collective-permute-start | bytes 786440 | tf_op jit(solution)/shard_map/ppermute | solution.py:199
  29.5 8.6 %collective-permute-start.6 = (bf16[16,32,256]{2,1,0:T(8,128)(2,1)S(1)}, bf16[16,32,256]{2,1,0:T(8,128)(2,1)S(1)}, u32[]{:S(2)}, u32[]{:S(2)}) collective-permute-start(bf16[16,32,256]{2,1,0:T(8,128)(2,1)S(1)} %collective-permute-done.5.refs_4_), channel_id=1, source_target_pairs={{0,1},{1,0},{2,3},{3,2},{4,5},{5,4},{6,7},{7,6},{8,9},{9,8},{10,11... | collective-permute-start | bytes 786440 | tf_op jit(solution)/shard_map/ppermute | solution.py:199
  31.6 6.5 %collective-permute-start.8 = (bf16[16,32,256]{2,1,0:T(8,128)(2,1)S(1)}, bf16[16,32,256]{2,1,0:T(8,128)(2,1)S(1)}, u32[]{:S(2)}, u32[]{:S(2)}) collective-permute-start(bf16[16,32,256]{2,1,0:T(8,128)(2,1)S(1)} %collective-permute-done.7.refs_6_), channel_id=1, source_target_pairs={{0,1},{1,0},{2,3},{3,2},{4,5},{5,4},{6,7},{7,6},{8,9},{9,8},{10,11... | collective-permute-start | bytes 786440 | tf_op jit(solution)/shard_map/ppermute | solution.py:199

commit v5 on v4

--- a/solution.py
+++ b/solution.py
@@ -10,7 +10,7 @@
 NEED = 4
 ITERS = 3
 TURN = 4
-ORDER = (4, 2, 6)
+ORDER = (4, 5, 2, 3, 6, 7, 1)
 
 
 def in_hbm(x):
@@ -76,12 +76,11 @@
 
 
 def first_pack_kernel(own_ref, asked_ref, rounded_ref, other_ref, *out_refs):
-    for r in range(asked_ref.shape[0]):
-        out_ref, at = (out_refs[r], 0) if r < 2 else (out_refs[r // 2 + 1], r % 2 * 2 * NEED)
-        g = (own_ref[0] % asked_ref.shape[0]) ^ r
+    for r, out_ref in enumerate(out_refs):
+        g = (own_ref[0] % len(out_refs)) ^ r
         for k in range(NEED):
-            out_ref[at + k] = rounded_ref[asked_ref[g, k]]
-            out_ref[at + NEED + k] = other_ref[asked_ref[g, NEED + k]]
+            out_ref[k] = rounded_ref[asked_ref[g, k]]
+            out_ref[NEED + k] = other_ref[asked_ref[g, NEED + k]]
 
 
 def turn_kernel(tiles_ref, out_ref, buf, sems):
@@ -128,9 +127,8 @@
 def first_step_kernel(place_ref, row_ref, own_ref, asked_ref, far_ref, *refs):
     arrived_refs, (decay_ref, seeds_ref, tiles_ref, out_ref, arrived, acc, blocks) = refs[:-7], refs[-7:]
     each = 2 * NEED
-    for r in range(arrived.shape[0] // each):
-        ref, at = (arrived_refs[r], 0) if r < 2 else (arrived_refs[r], r % 2 * each)
-        arrived[r * each:(r + 1) * each] = ref[at:at + each]
+    for r, ref in enumerate(arrived_refs):
+        arrived[r * each:(r + 1) * each] = ref[...]
     products(place_ref, row_ref, arrived, tiles_ref, acc)
     update(own_ref, asked_ref, far_ref, decay_ref, seeds_ref, out_ref, acc, blocks)
 
@@ -211,12 +209,9 @@
     other = away(rounded, group)
     asked = lax.all_to_all(wanted, "row", split_axis=0, concat_axis=0, tiled=True, axis_index_groups=halves)
     asked = asked.reshape(group, 2 * NEED)
-    chip = shape((2 * NEED, seed_count, TILE), jnp.bfloat16)
-    pair = shape((4 * NEED, seed_count, TILE), jnp.bfloat16)
-    chips = group // 2
     sent = pl.pallas_call(
-        first_pack_kernel, out_shape=(chip, chip) + (pair,) * (chips - 1),
-        in_specs=[smem, smem, vmem, vmem], out_specs=(vmem,) * (chips + 1),
+        first_pack_kernel, out_shape=(shape((2 * NEED, seed_count, TILE), jnp.bfloat16),) * group,
+        in_specs=[smem, smem, vmem, vmem], out_specs=(vmem,) * group,
         compiler_params=small, name="first_pack",
     )(own, asked, rounded, other)
     tiles, *sent = lax.optimization_barrier((tiles, *sent))
@@ -226,14 +221,10 @@
         compiler_params=pltpu.CompilerParams(vmem_limit_bytes=12 * mib), name="turn_tiles",
         cost_estimate=pl.CostEstimate(flops=6_000_000_000, bytes_accessed=8 * mib, transcendentals=0),
     )(in_hbm(tiles))
-    direct = []
+    arrived = {0: sent[0]}
     for r in ORDER:
-        direct.append(away(sent[r // 2 + 1], r))
+        arrived[r] = away(sent[r], r)
     far = away(asked, group)
-    arrived = {0: sent[0], 1: away(sent[1], 1)}
-    for r, x in zip(ORDER, direct):
-        arrived[r] = x
-        arrived[r + 1] = away(x, 1)
     outgoing = pl.pallas_call(
         first_step_kernel, out_shape=packed, in_specs=[smem] * 5 + [vmem] * (group + 3), out_specs=vmem,
         scratch_shapes=[pltpu.VMEM(packed.shape, packed.dtype), acc, blocks], compiler_params=small, name="first_step",

time: 97.8 us -> 97.9 us (level)
  starting transfers between devices: 16.1 us -> 13.9 us
  blocking collectives: 61 us -> 62.3 us
  waiting for transfers between devices: 5.48 us -> 6.48 us
    ppermute x9, starting transfers between devices: 16.1 us -> 13.9 us  [away(): return lax.ppermute(x, 'row', [(p, p ^ r) for p in range(panels)])]
    all_to_all x2, blocking collectives: 40.5 us -> 41.8 us  [per_device(): lax.all_to_all(outgoing, 'row', split_axis=0, concat_axis=0, tiled=True)]
    ppermute x9, waiting for transfers between devices: 5.48 us -> 6.48 us  [away(): return lax.ppermute(x, 'row', [(p, p ^ r) for p in range(panels)])]
where the time goes in v5:
time: 97.9 us; the launch traced here: 97.7 us
  blocking collectives  62.3 us (64%)
  Pallas kernels  14.3 us (15%)
  starting transfers between devices  13.9 us (14%)
  waiting for transfers between devices  6.48 us (7%)
    all_to_all x2, blocking collectives, per_device(): lax.all_to_all(outgoing, 'row', split_axis=0, concat_axis=0, tiled=True)  41.8 us
    ppermute x9, starting transfers between devices, away(): return lax.ppermute(x, 'row', [(p, p ^ r) for p in range(panels)])  13.9 us
    all_to_all x1, blocking collectives, per_device(): lax.all_to_all(squares, 'row', split_axis=0, concat_axis=0, tiled=True)  10.9 us
    all_to_all x1, blocking collectives, per_device(): lax.all_to_all(wanted, 'row', split_axis=0, concat_axis=0, tiled=True, ax...  9.64 us
    ppermute x9, waiting for transfers between devices, away(): return lax.ppermute(x, 'row', [(p, p ^ r) for p in range(panels)])  6.48 us
    pallas_call x1, Pallas kernels, per_device(): pl.pallas_call(turn_kernel, out_shape=shape(tiles.shape, tiles.dtype), in...  4.34 us
    pallas_call x1, Pallas kernels, per_device(): pl.pallas_call(first_step_kernel, out_shape=packed, in_specs=[smem] * 5 +...  2.45 us
    pallas_call x1, Pallas kernels, per_device(): pl.pallas_call(step_kernel, out_shape=packed, in_specs=[smem] * 5 + [vmem...  2.38 us
  transfers between devices with their start and end apart: 9, of which 3 were waited for; matrix products, arithmetic and copies ran while one was open for 0% of the time, Pallas kernels for 4%

profile of v5, /device:TPU:1, one launch (start us, length us, event | category | flops | bytes accessed | tf_op | source)
XLA Modules:
  0.0 97.7 jit_solution(9207294352002762352)
XLA Ops:
  0.7 1.2 %index.1 = (s32[8,1,8]{2,1,0:T(1,128)S(1)}, s32[1,64]{1,0:T(1,128)S(1)}, s32[1,64]{1,0:T(1,128)S(1)}, s32[1,64]{1,0:T(1,128)S(1)}, f32[32,1]{1,0:T(8,128)S(1)}, /*index=5*/bf16[16,32,256]{2,1,0:T(8,128)(2,1)S(1)}) custom-call(s32[1]{0:T(128)S(6)} %copy.7.count_ref, s32[1]{0:T(128)} %bitcast.own_ref, s32[1,64]{1,0:T(1,128)} %bitcast.9, s32[1,64]{1,0:T(1,128)} %bitcast.10, ...), custom_call_target="tpu_custom_call" | custom-call | tf_op jit(solution)/shard_map/index/pallas_call | solution.py:199
  1.8 3.8 %collective-permute-start.1 = (bf16[16,32,256]{2,1,0:T(8,128)(2,1)S(1)}, bf16[16,32,256]{2,1,0:T(8,128)(2,1)S(1)}, u32[]{:S(2)}, u32[]{:S(2)}) collective-permute-start(bf16[16,32,256]{2,1,0:T(8,128)(2,1)S(1)} %get-tuple-element.34.rounded_ref), channel_id=1, source_target_pairs={{0,8},{1,9},{2,10},{3,11},{4,12},{5,13},{6,14},{7,15},{8,0},{9,1},... | collective-permute-start | bytes 786440 | tf_op jit(solution)/shard_map/ppermute | solution.py:197
  5.6 9.6 %all_to_all.20 = s32[8,1,8]{2,1,0:T(1,128)S(1)} all-to-all(s32[8,1,8]{2,1,0:T(1,128)S(1)} %get-tuple-element.32), channel_id=1, replica_groups={{0,1,2,3,4,5,6,7},{8,9,10,11,12,13,14,15},{16,17,18,19,20,21,22,23},{24..., dimensions={0} | all-to-all | bytes 512 | tf_op jit(solution)/shard_map/all_to_all | solution.py:210
  15.3 0.0 collective-permute-done.1.other_ref
  15.3 0.7 first_pack.1
  16.0 0.0 copy-start
  16.0 0.8 collective-permute-start.2
  16.8 0.3 collective-permute-start.3
  17.0 0.8 collective-permute-start
  17.9 1.0 collective-permute-start.4
  18.8 2.6 %collective-permute-start.5 = (bf16[8,32,256]{2,1,0:T(8,128)(2,1)S(1)}, bf16[8,32,256]{2,1,0:T(8,128)(2,1)S(1)}, u32[]{:S(2)}, u32[]{:S(2)}) collective-permute-start(bf16[8,32,256]{2,1,0:T(8,128)(2,1)S(1)} %get-tuple-element.47), channel_id=1, source_target_pairs={{0,4},{1,5},{2,6},{3,7},{4,0},{5,1},{6,2},{7,3},{8,12},{9,13},{10,... | collective-permute-start | bytes 393224 | tf_op jit(solution)/shard_map/ppermute | solution.py:197
  21.4 0.0 collective-permute-done.far_ref
  21.4 2.8 %collective-permute-start.6 = (bf16[8,32,256]{2,1,0:T(8,128)(2,1)S(1)}, bf16[8,32,256]{2,1,0:T(8,128)(2,1)S(1)}, u32[]{:S(2)}, u32[]{:S(2)}) collective-permute-start(bf16[8,32,256]{2,1,0:T(8,128)(2,1)S(1)} %get-tuple-element.48), channel_id=1, source_target_pairs={{0,5},{1,4},{2,7},{3,6},{4,1},{5,0},{6,3},{7,2},{8,13},{9,12},{10,... | collective-permute-start | bytes 393224 | tf_op jit(solution)/shard_map/ppermute | solution.py:197
  24.2 0.0 collective-permute-done.2.refs_1_
  24.2 1.8 %collective-permute-start.7 = (bf16[8,32,256]{2,1,0:T(8,128)(2,1)S(1)}, bf16[8,32,256]{2,1,0:T(8,128)(2,1)S(1)}, u32[]{:S(2)}, u32[]{:S(2)}) collective-permute-start(bf16[8,32,256]{2,1,0:T(8,128)(2,1)S(1)} %get-tuple-element.49), channel_id=1, source_target_pairs={{0,6},{1,7},{2,4},{3,5},{4,2},{5,3},{6,0},{7,1},{8,14},{9,15},{10,... | collective-permute-start | bytes 393224 | tf_op jit(solution)/shard_map/ppermute | solution.py:197
  26.0 0.0 collective-permute-done.3.refs_2_
  26.0 0.0 collective-permute-start.8
  26.0 4.3 %turn_tiles.1.refs_10_.tiles_ref = bf16[64,256,256]{2,1,0:T(8,128)(2,1)S(1)} custom-call(bf16[64,256,256]{2,1,0:T(8,128)(2,1)} %tiles_ref), custom_call_target="tpu_custom_call" | custom-call | flops 6000000000 | bytes 8388608 | tf_op jit(solution)/shard_map/turn_tiles/pallas_call | solution.py:218
  30.4 0.0 collective-permute-done.4.refs_3_
  30.4 0.0 collective-permute-done.5.refs_4_
  30.4 0.7 collective-permute-done.6.refs_5_
  31.1 2.9 %collective-permute-done.7.refs_6_ = bf16[8,32,256]{2,1,0:T(8,128)(2,1)S(1)} collective-permute-done((bf16[8,32,256]{2,1,0:T(8,128)(2,1)S(1)}, bf16[8,32,256]{2,1,0:T(8,128)(2,1)S(1)}, u32[]{:S(2)}, u32[]{:S(2)}) %collective-permute-start.7) | collective-permute-done | bytes 131104 | tf_op jit(solution)/shard_map/ppermute | solution.py:197
  34.1 2.8 %collective-permute-done.8.refs_7_ = bf16[8,32,256]{2,1,0:T(8,128)(2,1)S(1)} collective-permute-done((bf16[8,32,256]{2,1,0:T(8,128)(2,1)S(1)}, bf16[8,32,256]{2,1,0:T(8,128)(2,1)S(1)}, u32[]{:S(2)}, u32[]{:S(2)}) %collective-permute-start.8) | collective-permute-done | bytes 131104 | tf_op jit(solution)/shard_map/ppermute | solution.py:197
  36.9 0.0 copy-done
  36.9 2.5 %first_step.1 = bf16[64,32,256]{2,1,0:T(8,128)(2,1)S(1)} custom-call(s32[1,64]{1,0:T(1,128)S(1)} %get-tuple-element.33.place_ref, s32[1,64]{1,0:T(1,128)S(1)} %get-tuple-element.31.row_ref, s32[1]{0:T(128)} %bitcast.own_ref, s32[8,8]{1,0:T(8,128)S(1)} %bitcast.7, s32[8,8]{1,0:T(8,128)S(1)} %collective-permute-done.far_ref, ...), custom_call_target="tpu_custom_call" | custom-call | tf_op jit(solution)/shard_map/first_step/pallas_call | solution.py:228
  39.3 21.2 %all_to_all.21.arrived_ref = bf16[64,32,256]{2,1,0:T(8,128)(2,1)S(1)} all-to-all(bf16[64,32,256]{2,1,0:T(8,128)(2,1)S(1)} %first_step.1), channel_id=1, replica_groups=mesh['graph'=16,'row'=16] {'row'}, dimensions={0} | all-to-all | bytes 2097152 | tf_op jit(solution)/shard_map/all_to_all | solution.py:233
  60.5 2.4 %step.1 = bf16[64,32,256]{2,1,0:T(8,128)(2,1)S(1)} custom-call(s32[1,64]{1,0:T(1,128)S(1)} %get-tuple-element.30.place_ref, s32[1,64]{1,0:T(1,128)S(1)} %get-tuple-element.31.row_ref, s32[1]{0:T(128)} %bitcast.own_ref, s32[8,8]{1,0:T(8,128)S(1)} %bitcast.8, s32[8,8]{1,0:T(8,128)S(1)} %collective-permute-done.far_ref, ...), custom_call_target="tpu_custom_call" | custom-call | tf_op jit(solution)/shard_map/step/pallas_call | solution.py:235
  62.9 20.6 %all_to_all.22.arrived_ref = bf16[64,32,256]{2,1,0:T(8,128)(2,1)S(1)} all-to-all(bf16[64,32,256]{2,1,0:T(8,128)(2,1)S(1)} %step.1), channel_id=1, replica_groups=mesh['graph'=16,'row'=16] {'row'}, dimensions={0} | all-to-all | bytes 2097152 | tf_op jit(solution)/shard_map/all_to_all | solution.py:233
  83.5 2.3 %last.1 = (f32[32,4096]{1,0:T(8,128)S(1)}, f32[16,1,32]{2,1,0:T(1,128)S(1)}) custom-call(s32[1,64]{1,0:T(1,128)S(1)} %get-tuple-element.30.place_ref, s32[1,64]{1,0:T(1,128)S(1)} %get-tuple-element.31.row_ref, bf16[64,32,256]{2,1,0:T(8,128)(2,1)S(1)} %all_to_all.22.arrived_ref, f32[32,1]{1,0:T(8,128)S(1)} %get-tuple-element.51.refs_8_.decay_ref, ...), custom_call_target="tpu_custom_call" | custom-call | tf_op jit(solution)/shard_map/last/pallas_call | solution.py:240
  85.8 10.9 %all_to_all.23.squares_ref = f32[16,1,32]{2,1,0:T(1,128)S(1)} all-to-all(f32[16,1,32]{2,1,0:T(1,128)S(1)} %get-tuple-element.53), channel_id=1, replica_groups=mesh['graph'=16,'row'=16] {'row'}, dimensions={0} | all-to-all | bytes 4096 | tf_op jit(solution)/shard_map/all_to_all | solution.py:245
  96.7 0.9 scale.1
Async XLA Ops:
  1.8 13.5 %collective-permute-start.1 = (bf16[16,32,256]{2,1,0:T(8,128)(2,1)S(1)}, bf16[16,32,256]{2,1,0:T(8,128)(2,1)S(1)}, u32[]{:S(2)}, u32[]{:S(2)}) collective-permute-start(bf16[16,32,256]{2,1,0:T(8,128)(2,1)S(1)} %get-tuple-element.34.rounded_ref), channel_id=1, source_target_pairs={{0,8},{1,9},{2,10},{3,11},{4,12},{5,13},{6,14},{7,15},{8,0},{9,1},... | collective-permute-start | bytes 786440 | tf_op jit(solution)/shard_map/ppermute | solution.py:197
  16.0 20.9 %copy-start = (f32[32,4096]{1,0:T(8,128)S(1)}, f32[32,4096]{1,0:T(8,128)}, u32[]{:S(2)}) copy-start(f32[32,4096]{1,0:T(8,128)} %seeds_ref.5) | copy-start | bytes 1572868
  16.0 8.2 %collective-permute-start.2 = (bf16[8,32,256]{2,1,0:T(8,128)(2,1)S(1)}, bf16[8,32,256]{2,1,0:T(8,128)(2,1)S(1)}, u32[]{:S(2)}, u32[]{:S(2)}) collective-permute-start(bf16[8,32,256]{2,1,0:T(8,128)(2,1)S(1)} %get-tuple-element.44), channel_id=1, source_target_pairs={{0,1},{1,0},{2,3},{3,2},{4,5},{5,4},{6,7},{7,6},{8,9},{9,8},{10,11... | collective-permute-start | bytes 393224 | tf_op jit(solution)/shard_map/ppermute | solution.py:197
  16.8 9.2 %collective-permute-start.3 = (bf16[8,32,256]{2,1,0:T(8,128)(2,1)S(1)}, bf16[8,32,256]{2,1,0:T(8,128)(2,1)S(1)}, u32[]{:S(2)}, u32[]{:S(2)}) collective-permute-start(bf16[8,32,256]{2,1,0:T(8,128)(2,1)S(1)} %get-tuple-element.45), channel_id=1, source_target_pairs={{0,2},{1,3},{2,0},{3,1},{4,6},{5,7},{6,4},{7,5},{8,10},{9,11},{10,... | collective-permute-start | bytes 393224 | tf_op jit(solution)/shard_map/ppermute | solution.py:197
  17.0 4.4 %collective-permute-start = (s32[8,8]{1,0:T(8,128)S(1)}, s32[8,8]{1,0:T(8,128)S(1)}, u32[]{:S(2)}, u32[]{:S(2)}) collective-permute-start(s32[8,8]{1,0:T(8,128)S(1)} %bitcast.6), channel_id=1, source_target_pairs={{0,8},{1,9},{2,10},{3,11},{4,12},{5,13},{6,14},{7,15},{8,0},{9,1},... | collective-permute-start | bytes 776 | tf_op jit(solution)/shard_map/ppermute | solution.py:197
  17.9 12.5 %collective-permute-start.4 = (bf16[8,32,256]{2,1,0:T(8,128)(2,1)S(1)}, bf16[8,32,256]{2,1,0:T(8,128)(2,1)S(1)}, u32[]{:S(2)}, u32[]{:S(2)}) collective-permute-start(bf16[8,32,256]{2,1,0:T(8,128)(2,1)S(1)} %get-tuple-element.46), channel_id=1, source_target_pairs={{0,3},{1,2},{2,1},{3,0},{4,7},{5,6},{6,5},{7,4},{8,11},{9,10},{10,... | collective-permute-start | bytes 393224 | tf_op jit(solution)/shard_map/ppermute | solution.py:197
  18.8 11.6 %collective-permute-start.5 = (bf16[8,32,256]{2,1,0:T(8,128)(2,1)S(1)}, bf16[8,32,256]{2,1,0:T(8,128)(2,1)S(1)}, u32[]{:S(2)}, u32[]{:S(2)}) collective-permute-start(bf16[8,32,256]{2,1,0:T(8,128)(2,1)S(1)} %get-tuple-element.47), channel_id=1, source_target_pairs={{0,4},{1,5},{2,6},{3,7},{4,0},{5,1},{6,2},{7,3},{8,12},{9,13},{10,... | collective-permute-start | bytes 393224 | tf_op jit(solution)/shard_map/ppermute | solution.py:197
  21.4 9.7 %collective-permute-start.6 = (bf16[8,32,256]{2,1,0:T(8,128)(2,1)S(1)}, bf16[8,32,256]{2,1,0:T(8,128)(2,1)S(1)}, u32[]{:S(2)}, u32[]{:S(2)}) collective-permute-start(bf16[8,32,256]{2,1,0:T(8,128)(2,1)S(1)} %get-tuple-element.48), channel_id=1, source_target_pairs={{0,5},{1,4},{2,7},{3,6},{4,1},{5,0},{6,3},{7,2},{8,13},{9,12},{10,... | collective-permute-start | bytes 393224 | tf_op jit(solution)/shard_map/ppermute | solution.py:197
  24.2 9.9 %collective-permute-start.7 = (bf16[8,32,256]{2,1,0:T(8,128)(2,1)S(1)}, bf16[8,32,256]{2,1,0:T(8,128)(2,1)S(1)}, u32[]{:S(2)}, u32[]{:S(2)}) collective-permute-start(bf16[8,32,256]{2,1,0:T(8,128)(2,1)S(1)} %get-tuple-element.49), channel_id=1, source_target_pairs={{0,6},{1,7},{2,4},{3,5},{4,2},{5,3},{6,0},{7,1},{8,14},{9,15},{10,... | collective-permute-start | bytes 393224 | tf_op jit(solution)/shard_map/ppermute | solution.py:197
  26.0 10.9 %collective-permute-start.8 = (bf16[8,32,256]{2,1,0:T(8,128)(2,1)S(1)}, bf16[8,32,256]{2,1,0:T(8,128)(2,1)S(1)}, u32[]{:S(2)}, u32[]{:S(2)}) collective-permute-start(bf16[8,32,256]{2,1,0:T(8,128)(2,1)S(1)} %get-tuple-element.50), channel_id=1, source_target_pairs={{0,7},{1,6},{2,5},{3,4},{4,3},{5,2},{6,1},{7,0},{8,15},{9,14},{10,... | collective-permute-start | bytes 393224 | tf_op jit(solution)/shard_map/ppermute | solution.py:197

commit v6 on v5

--- a/solution.py
+++ b/solution.py
@@ -10,6 +10,7 @@
 NEED = 4
 ITERS = 3
 TURN = 4
+FAR = 4
 ORDER = (4, 5, 2, 3, 6, 7, 1)
 
 
@@ -58,7 +59,9 @@
     side = jnp.where((panel >= group) == (half == 1), 0, NEED)
     away = (panel % group) ^ own
     shift = (away * 2 * NEED + side - panel * NEED).astype(jnp.float32)
-    near_spot = jnp.where(local >= 0, jnp.where(local < blk, spot + shift, 0.0), 0.0)
+    whole = (away >= FAR) & (away < FAR + 2) & (side == 0)
+    behind = (panels * NEED + (away - FAR) * blk + local).astype(jnp.float32)
+    near_spot = jnp.where((local >= 0) & (local < blk), jnp.where(whole, behind, spot + shift), 0.0)
     near_place_ref[...] = jnp.sum(near_spot, axis=0, keepdims=True).astype(jnp.int32)
     gets[1].wait()
     row_ref[...] = jnp.where(live[:1], rows_v[...], blk)
@@ -78,27 +81,20 @@
 def first_pack_kernel(own_ref, asked_ref, rounded_ref, other_ref, *out_refs):
     for r, out_ref in enumerate(out_refs):
         g = (own_ref[0] % len(out_refs)) ^ r
+        skip = out_ref.shape[0] - NEED
         for k in range(NEED):
-            out_ref[k] = rounded_ref[asked_ref[g, k]]
-            out_ref[NEED + k] = other_ref[asked_ref[g, NEED + k]]
-
-
-def turn_kernel(tiles_ref, out_ref, buf, sems):
-    chunk = buf.shape[0] // sems.shape[0]
-    parts = [pl.ds(c * chunk, chunk) for c in range(sems.shape[0])]
-    gets = [pltpu.make_async_copy(tiles_ref.at[p], buf.at[p], sems.at[c]) for c, p in enumerate(parts)]
-    for get in gets:
-        get.start()
-    for c, get in enumerate(gets):
-        get.wait()
-
-        def body(i, carry, c=c):
-            for k in range(TURN):
-                t = c * chunk + i * TURN + k
-                out_ref[t] = buf[t].T
-            return carry
-
-        lax.fori_loop(0, chunk // TURN, body, 0)
+            if skip:
+                out_ref[k] = rounded_ref[asked_ref[g, k]]
+            out_ref[skip + k] = other_ref[asked_ref[g, NEED + k]]
+
+
+def turn_kernel(tiles_ref, out_ref):
+    def body(i, carry):
+        for k in range(TURN):
+            out_ref[i * TURN + k] = tiles_ref[i * TURN + k].T
+        return carry
+
+    lax.fori_loop(0, tiles_ref.shape[0] // TURN, body, 0)
 
 
 def send_blocks(blocks, own_ref, asked_ref, far_ref, out_ref):
@@ -127,8 +123,12 @@
 def first_step_kernel(place_ref, row_ref, own_ref, asked_ref, far_ref, *refs):
     arrived_refs, (decay_ref, seeds_ref, tiles_ref, out_ref, arrived, acc, blocks) = refs[:-7], refs[-7:]
     each = 2 * NEED
-    for r, ref in enumerate(arrived_refs):
-        arrived[r * each:(r + 1) * each] = ref[...]
+    at = 0
+    for ref in arrived_refs:
+        count = ref.shape[0]
+        at += each - count if count < each else 0
+        arrived[at:at + count] = ref[...]
+        at += count
     products(place_ref, row_ref, arrived, tiles_ref, acc)
     update(own_ref, asked_ref, far_ref, decay_ref, seeds_ref, out_ref, acc, blocks)
 
@@ -207,28 +207,31 @@
     )(tile_count, own, in_hbm(tile_cols.reshape(1, slots)), in_hbm(tile_rows.reshape(1, slots)),
       in_hbm(decay.reshape(1, seed_count)), in_hbm(seeds))
     other = away(rounded, group)
+    cross = away(rounded, FAR)
     asked = lax.all_to_all(wanted, "row", split_axis=0, concat_axis=0, tiled=True, axis_index_groups=halves)
     asked = asked.reshape(group, 2 * NEED)
     sent = pl.pallas_call(
-        first_pack_kernel, out_shape=(shape((2 * NEED, seed_count, TILE), jnp.bfloat16),) * group,
+        first_pack_kernel, out_shape=tuple(shape(((1 if r // 2 * 2 == FAR else 2) * NEED, seed_count, TILE), jnp.bfloat16)
+                                           for r in range(group)),
         in_specs=[smem, smem, vmem, vmem], out_specs=(vmem,) * group,
         compiler_params=small, name="first_pack",
+        cost_estimate=pl.CostEstimate(flops=20_000_000_000, bytes_accessed=2 * mib, transcendentals=0),
     )(own, asked, rounded, other)
     tiles, *sent = lax.optimization_barrier((tiles, *sent))
     turned = pl.pallas_call(
-        turn_kernel, out_shape=shape(tiles.shape, tiles.dtype), in_specs=[hbm], out_specs=vmem,
-        scratch_shapes=[pltpu.VMEM(tiles.shape, tiles.dtype), dma((8,))],
-        compiler_params=pltpu.CompilerParams(vmem_limit_bytes=12 * mib), name="turn_tiles",
+        turn_kernel, out_shape=shape(tiles.shape, tiles.dtype), in_specs=[vmem], out_specs=vmem,
+        compiler_params=small, name="turn_tiles",
         cost_estimate=pl.CostEstimate(flops=6_000_000_000, bytes_accessed=8 * mib, transcendentals=0),
-    )(in_hbm(tiles))
+    )(tiles)
     arrived = {0: sent[0]}
     for r in ORDER:
         arrived[r] = away(sent[r], r)
     far = away(asked, group)
+    crossed = away(cross, 1)
     outgoing = pl.pallas_call(
-        first_step_kernel, out_shape=packed, in_specs=[smem] * 5 + [vmem] * (group + 3), out_specs=vmem,
-        scratch_shapes=[pltpu.VMEM(packed.shape, packed.dtype), acc, blocks], compiler_params=small, name="first_step",
-    )(near_place, row, own, asked, far, *[arrived[r] for r in range(group)], column, seeds, turned)
+        first_step_kernel, out_shape=packed, in_specs=[smem] * 5 + [vmem] * (group + 5), out_specs=vmem,
+        scratch_shapes=[pltpu.VMEM((bufs + 2 * blk, seed_count, TILE), packed.dtype), acc, blocks], compiler_params=small, name="first_step",
+    )(near_place, row, own, asked, far, *[arrived[r] for r in range(group)], cross, crossed, column, seeds, turned)
     for step in range(1, ITERS):
         arrived = lax.all_to_all(outgoing, "row", split_axis=0, concat_axis=0, tiled=True)
         if step < ITERS - 1:

time: 97.9 us -> 97.1 us (level)
  blocking collectives: 62.3 us -> 52.6 us
  starting transfers between devices: 13.9 us -> 22.6 us
    all_to_all x1 -> x0, blocking collectives: 9.64 us -> none  [per_device(): lax.all_to_all(wanted, 'row', split_axis=0, concat_axis=0, tiled=True, ax...]
    all_to_all x0 -> x1, starting transfers between devices: none -> 5.25 us  [per_device(): lax.all_to_all(wanted, 'row', split_axis=0, concat_axis=0, tiled=True, ax...]
    ppermute x9 -> x11, starting transfers between devices: 13.9 us -> 17.4 us  [away(): return lax.ppermute(x, 'row', [(p, p ^ r) for p in range(panels)])]
    all_to_all x0 -> x1, waiting for transfers between devices: none -> 1.68 us  [per_device(): lax.all_to_all(wanted, 'row', split_axis=0, concat_axis=0, tiled=True, ax...]
    pallas_call x1, Pallas kernels: 4.34 us -> 3.03 us  [per_device(): pl.pallas_call(turn_kernel, out_shape=shape(tiles.shape, tiles.dtype), in...]
    ppermute x9 -> x11, waiting for transfers between devices: 6.48 us -> 5.61 us  [away(): return lax.ppermute(x, 'row', [(p, p ^ r) for p in range(panels)])]
  transfers between devices with their start and end apart: 9 -> 12, of which waited for: 3 -> 4; matrix products, arithmetic and copies ran while one was open for 0% -> 0% of each run, Pallas kernels for 4% -> 4%
where the time goes in v6:
time: 97.1 us; the launch traced here: 96.8 us
  blocking collectives  52.6 us (54%)
  starting transfers between devices  22.6 us (23%)
  Pallas kernels  13.6 us (14%)
  waiting for transfers between devices  7.29 us (8%)
    all_to_all x2, blocking collectives, per_device(): lax.all_to_all(outgoing, 'row', split_axis=0, concat_axis=0, tiled=True)  41.7 us
    ppermute x11, starting transfers between devices, away(): return lax.ppermute(x, 'row', [(p, p ^ r) for p in range(panels)])  17.4 us
    all_to_all x1, blocking collectives, per_device(): lax.all_to_all(squares, 'row', split_axis=0, concat_axis=0, tiled=True)  10.9 us
    ppermute x11, waiting for transfers between devices, away(): return lax.ppermute(x, 'row', [(p, p ^ r) for p in range(panels)])  5.61 us
    all_to_all x1, starting transfers between devices, per_device(): lax.all_to_all(wanted, 'row', split_axis=0, concat_axis=0, tiled=True, ax...  5.25 us
    pallas_call x1, Pallas kernels, per_device(): pl.pallas_call(turn_kernel, out_shape=shape(tiles.shape, tiles.dtype), in...  3.03 us
    pallas_call x1, Pallas kernels, per_device(): pl.pallas_call(first_step_kernel, out_shape=packed, in_specs=[smem] * 5 +...  2.48 us
    pallas_call x1, Pallas kernels, per_device(): pl.pallas_call(step_kernel, out_shape=packed, in_specs=[smem] * 5 + [vmem...  2.38 us
  transfers between devices with their start and end apart: 12, of which 4 were waited for; matrix products, arithmetic and copies ran while one was open for 0% of the time, Pallas kernels for 4%

profile of v6, /device:TPU:1, one launch (start us, length us, event | category | flops | bytes accessed | tf_op | source)
XLA Modules:
  0.0 96.8 jit_solution(13671556047461263879)
XLA Ops:
  0.7 1.7 %index.1 = (s32[8,1,8]{2,1,0:T(1,128)}, s32[1,64]{1,0:T(1,128)S(1)}, s32[1,64]{1,0:T(1,128)S(1)}, s32[1,64]{1,0:T(1,128)S(1)}, f32[32,1]{1,0:T(8,128)S(1)}, /*index=5*/bf16[16,32,256]{2,1,0:T(8,128)(2,1)S(1)}) custom-call(s32[1]{0:T(128)S(6)} %copy.7.count_ref, s32[1]{0:T(128)} %bitcast.own_ref, s32[1,64]{1,0:T(1,128)} %bitcast.9, s32[1,64]{1,0:T(1,128)} %bitcast.10, ...), custom_call_target="tpu_custom_call" | custom-call | tf_op jit(solution)/shard_map/index/pallas_call | solution.py:199
  2.4 3.8 %collective-permute-start.1 = (bf16[16,32,256]{2,1,0:T(8,128)(2,1)S(1)}, bf16[16,32,256]{2,1,0:T(8,128)(2,1)S(1)}, u32[]{:S(2)}, u32[]{:S(2)}) collective-permute-start(bf16[16,32,256]{2,1,0:T(8,128)(2,1)S(1)} %get-tuple-element.34.rounded_ref), channel_id=1, source_target_pairs={{0,8},{1,9},{2,10},{3,11},{4,12},{5,13},{6,14},{7,15},{8,0},{9,1},... | collective-permute-start | bytes 786440 | tf_op jit(solution)/shard_map/ppermute | solution.py:197
  6.2 5.3 %all-to-all-start = ((s32[8,1,8]{2,1,0:T(1,128)}), s32[8,1,8]{2,1,0:T(1,128)S(1)}, u32[]{:S(2)}, u32[]{:S(2)}) async-start(s32[8,1,8]{2,1,0:T(1,128)} %get-tuple-element.32), calls=%async_computation | async-start | bytes 8192 | tf_op jit(solution)/shard_map/all_to_all | solution.py:211
  11.4 2.9 %collective-permute-start.9 = (bf16[16,32,256]{2,1,0:T(8,128)(2,1)S(1)}, bf16[16,32,256]{2,1,0:T(8,128)(2,1)S(1)}, u32[]{:S(2)}, u32[]{:S(2)}) collective-permute-start(bf16[16,32,256]{2,1,0:T(8,128)(2,1)S(1)} %get-tuple-element.34.rounded_ref), channel_id=1, source_target_pairs={{0,4},{1,5},{2,6},{3,7},{4,0},{5,1},{6,2},{7,3},{8,12},{9,13},{10,... | collective-permute-start | bytes 786440 | tf_op jit(solution)/shard_map/ppermute | solution.py:197
  14.3 1.7 %all-to-all-done = s32[8,1,8]{2,1,0:T(1,128)S(1)} async-done(((s32[8,1,8]{2,1,0:T(1,128)}), s32[8,1,8]{2,1,0:T(1,128)S(1)}, u32[]{:S(2)}, u32[]{:S(2)}) %all-to-all-start) | async-done | bytes 288 | tf_op jit(solution)/shard_map/all_to_all | solution.py:211
  16.0 0.0 collective-permute-done.1.other_ref
  16.0 0.0 copy-start.1
  16.0 0.7 first_pack.1
  16.7 0.0 copy-start
  16.7 0.8 collective-permute-start.2
  17.5 0.9 collective-permute-start.5
  18.3 2.4 %collective-permute-start.6 = (bf16[4,32,256]{2,1,0:T(8,128)(2,1)S(1)}, bf16[4,32,256]{2,1,0:T(8,128)(2,1)S(1)}, u32[]{:S(2)}, u32[]{:S(2)}) collective-permute-start(bf16[4,32,256]{2,1,0:T(8,128)(2,1)S(1)} %get-tuple-element.48), channel_id=1, source_target_pairs={{0,5},{1,4},{2,7},{3,6},{4,1},{5,0},{6,3},{7,2},{8,13},{9,12},{10,... | collective-permute-start | bytes 196616 | tf_op jit(solution)/shard_map/ppermute | solution.py:197
  20.7 0.7 collective-permute-start
  21.4 3.3 %collective-permute-done.far_ref = s32[8,8]{1,0:T(8,128)S(1)} collective-permute-done((s32[8,8]{1,0:T(8,128)S(1)}, s32[8,8]{1,0:T(8,128)S(1)}, u32[]{:S(2)}, u32[]{:S(2)}) %collective-permute-start) | collective-permute-done | bytes 288 | tf_op jit(solution)/shard_map/ppermute | solution.py:197
  24.7 0.3 collective-permute-start.3
  24.9 0.0 collective-permute-done.9.refs_8_
  24.9 2.6 %collective-permute-start.4 = (bf16[8,32,256]{2,1,0:T(8,128)(2,1)S(1)}, bf16[8,32,256]{2,1,0:T(8,128)(2,1)S(1)}, u32[]{:S(2)}, u32[]{:S(2)}) collective-permute-start(bf16[8,32,256]{2,1,0:T(8,128)(2,1)S(1)} %get-tuple-element.46), channel_id=1, source_target_pairs={{0,3},{1,2},{2,1},{3,0},{4,7},{5,6},{6,5},{7,4},{8,11},{9,10},{10,... | collective-permute-start | bytes 393224 | tf_op jit(solution)/shard_map/ppermute | solution.py:197
  27.6 0.0 collective-permute-done.5.refs_4_
  27.6 0.9 collective-permute-start.7
  28.5 0.0 collective-permute-done.6.refs_5_
  28.5 1.0 %collective-permute-start.8 = (bf16[8,32,256]{2,1,0:T(8,128)(2,1)S(1)}, bf16[8,32,256]{2,1,0:T(8,128)(2,1)S(1)}, u32[]{:S(2)}, u32[]{:S(2)}) collective-permute-start(bf16[8,32,256]{2,1,0:T(8,128)(2,1)S(1)} %get-tuple-element.50), channel_id=1, source_target_pairs={{0,7},{1,6},{2,5},{3,4},{4,3},{5,2},{6,1},{7,0},{8,15},{9,14},{10,... | collective-permute-start | bytes 393224 | tf_op jit(solution)/shard_map/ppermute | solution.py:197
  29.4 0.0 collective-permute-done.2.refs_1_
  29.4 1.2 %collective-permute-start.10 = (bf16[16,32,256]{2,1,0:T(8,128)(2,1)S(1)}, bf16[16,32,256]{2,1,0:T(8,128)(2,1)S(1)}, u32[]{:S(2)}, u32[]{:S(2)}) collective-permute-start(bf16[16,32,256]{2,1,0:T(8,128)(2,1)S(1)} %collective-permute-done.9.refs_8_), channel_id=1, source_target_pairs={{0,1},{1,0},{2,3},{3,2},{4,5},{5,4},{6,7},{7,6},{8,9},{9,8},{10,11... | collective-permute-start | bytes 786440 | tf_op jit(solution)/shard_map/ppermute | solution.py:197
  30.7 0.0 copy-done.1
  30.7 3.0 %turn_tiles.1.refs_12_.tiles_ref = bf16[64,256,256]{2,1,0:T(8,128)(2,1)S(1)} custom-call(bf16[64,256,256]{2,1,0:T(8,128)(2,1)S(1)} %copy-done.1), custom_call_target="tpu_custom_call" | custom-call | flops 6000000000 | bytes 8388608 | tf_op jit(solution)/shard_map/turn_tiles/pallas_call | solution.py:221
  33.7 0.0 collective-permute-done.3.refs_2_
  33.7 0.0 collective-permute-done.4.refs_3_
  33.7 0.3 collective-permute-done.7.refs_6_
  34.0 2.0 %collective-permute-done.8.refs_7_ = bf16[8,32,256]{2,1,0:T(8,128)(2,1)S(1)} collective-permute-done((bf16[8,32,256]{2,1,0:T(8,128)(2,1)S(1)}, bf16[8,32,256]{2,1,0:T(8,128)(2,1)S(1)}, u32[]{:S(2)}, u32[]{:S(2)}) %collective-permute-start.8) | collective-permute-done | bytes 131104 | tf_op jit(solution)/shard_map/ppermute | solution.py:197
  36.1 0.0 collective-permute-done.10.refs_9_
  36.1 0.0 copy-done
  36.1 2.5 %first_step.1 = bf16[64,32,256]{2,1,0:T(8,128)(2,1)S(1)} custom-call(s32[1,64]{1,0:T(1,128)S(1)} %get-tuple-element.33.place_ref, s32[1,64]{1,0:T(1,128)S(1)} %get-tuple-element.31.row_ref, s32[1]{0:T(128)} %bitcast.own_ref, s32[8,8]{1,0:T(8,128)S(1)} %bitcast.7, s32[8,8]{1,0:T(8,128)S(1)} %collective-permute-done.far_ref, ...), custom_call_target="tpu_custom_call" | custom-call | tf_op jit(solution)/shard_map/first_step/pallas_call | solution.py:231
  38.5 21.1 %all_to_all.20.arrived_ref = bf16[64,32,256]{2,1,0:T(8,128)(2,1)S(1)} all-to-all(bf16[64,32,256]{2,1,0:T(8,128)(2,1)S(1)} %first_step.1), channel_id=1, replica_groups=mesh['graph'=16,'row'=16] {'row'}, dimensions={0} | all-to-all | bytes 2097152 | tf_op jit(solution)/shard_map/all_to_all | solution.py:236
  59.7 2.4 %step.1 = bf16[64,32,256]{2,1,0:T(8,128)(2,1)S(1)} custom-call(s32[1,64]{1,0:T(1,128)S(1)} %get-tuple-element.30.place_ref, s32[1,64]{1,0:T(1,128)S(1)} %get-tuple-element.31.row_ref, s32[1]{0:T(128)} %bitcast.own_ref, s32[8,8]{1,0:T(8,128)S(1)} %bitcast.8, s32[8,8]{1,0:T(8,128)S(1)} %collective-permute-done.far_ref, ...), custom_call_target="tpu_custom_call" | custom-call | tf_op jit(solution)/shard_map/step/pallas_call | solution.py:238
  62.0 20.6 %all_to_all.21.arrived_ref = bf16[64,32,256]{2,1,0:T(8,128)(2,1)S(1)} all-to-all(bf16[64,32,256]{2,1,0:T(8,128)(2,1)S(1)} %step.1), channel_id=1, replica_groups=mesh['graph'=16,'row'=16] {'row'}, dimensions={0} | all-to-all | bytes 2097152 | tf_op jit(solution)/shard_map/all_to_all | solution.py:236
  82.6 2.3 %last.1 = (f32[32,4096]{1,0:T(8,128)S(1)}, f32[16,1,32]{2,1,0:T(1,128)S(1)}) custom-call(s32[1,64]{1,0:T(1,128)S(1)} %get-tuple-element.30.place_ref, s32[1,64]{1,0:T(1,128)S(1)} %get-tuple-element.31.row_ref, bf16[64,32,256]{2,1,0:T(8,128)(2,1)S(1)} %all_to_all.21.arrived_ref, f32[32,1]{1,0:T(8,128)S(1)} %get-tuple-element.51.refs_10_.decay_ref, ...), custom_call_target="tpu_custom_call" | custom-call | tf_op jit(solution)/shard_map/last/pallas_call | solution.py:243
  85.0 10.9 %all_to_all.22.squares_ref = f32[16,1,32]{2,1,0:T(1,128)S(1)} all-to-all(f32[16,1,32]{2,1,0:T(1,128)S(1)} %get-tuple-element.53), channel_id=1, replica_groups=mesh['graph'=16,'row'=16] {'row'}, dimensions={0} | all-to-all | bytes 4096 | tf_op jit(solution)/shard_map/all_to_all | solution.py:248
  95.9 0.9 scale.1
Async XLA Ops:
  2.4 13.6 %collective-permute-start.1 = (bf16[16,32,256]{2,1,0:T(8,128)(2,1)S(1)}, bf16[16,32,256]{2,1,0:T(8,128)(2,1)S(1)}, u32[]{:S(2)}, u32[]{:S(2)}) collective-permute-start(bf16[16,32,256]{2,1,0:T(8,128)(2,1)S(1)} %get-tuple-element.34.rounded_ref), channel_id=1, source_target_pairs={{0,8},{1,9},{2,10},{3,11},{4,12},{5,13},{6,14},{7,15},{8,0},{9,1},... | collective-permute-start | bytes 786440 | tf_op jit(solution)/shard_map/ppermute | solution.py:197
  6.2 9.8 %all-to-all-start = ((s32[8,1,8]{2,1,0:T(1,128)}), s32[8,1,8]{2,1,0:T(1,128)S(1)}, u32[]{:S(2)}, u32[]{:S(2)}) async-start(s32[8,1,8]{2,1,0:T(1,128)} %get-tuple-element.32), calls=%async_computation | async-start | bytes 8192 | tf_op jit(solution)/shard_map/all_to_all | solution.py:211
  11.4 13.5 %collective-permute-start.9 = (bf16[16,32,256]{2,1,0:T(8,128)(2,1)S(1)}, bf16[16,32,256]{2,1,0:T(8,128)(2,1)S(1)}, u32[]{:S(2)}, u32[]{:S(2)}) collective-permute-start(bf16[16,32,256]{2,1,0:T(8,128)(2,1)S(1)} %get-tuple-element.34.rounded_ref), channel_id=1, source_target_pairs={{0,4},{1,5},{2,6},{3,7},{4,0},{5,1},{6,2},{7,3},{8,12},{9,13},{10,... | collective-permute-start | bytes 786440 | tf_op jit(solution)/shard_map/ppermute | solution.py:197
  16.0 14.7 %copy-start.1 = (bf16[64,256,256]{2,1,0:T(8,128)(2,1)S(1)}, bf16[64,256,256]{2,1,0:T(8,128)(2,1)}, u32[]{:S(2)}) copy-start(bf16[64,256,256]{2,1,0:T(8,128)(2,1)} %tiles_ref) | copy-start | bytes 25165828
  16.7 19.4 %copy-start = (f32[32,4096]{1,0:T(8,128)S(1)}, f32[32,4096]{1,0:T(8,128)}, u32[]{:S(2)}) copy-start(f32[32,4096]{1,0:T(8,128)} %seeds_ref.5) | copy-start | bytes 1572868
  16.7 12.8 %collective-permute-start.2 = (bf16[8,32,256]{2,1,0:T(8,128)(2,1)S(1)}, bf16[8,32,256]{2,1,0:T(8,128)(2,1)S(1)}, u32[]{:S(2)}, u32[]{:S(2)}) collective-permute-start(bf16[8,32,256]{2,1,0:T(8,128)(2,1)S(1)} %get-tuple-element.44), channel_id=1, source_target_pairs={{0,1},{1,0},{2,3},{3,2},{4,5},{5,4},{6,7},{7,6},{8,9},{9,8},{10,11... | collective-permute-start | bytes 393224 | tf_op jit(solution)/shard_map/ppermute | solution.py:197
  17.5 10.1 %collective-permute-start.5 = (bf16[4,32,256]{2,1,0:T(8,128)(2,1)S(1)}, bf16[4,32,256]{2,1,0:T(8,128)(2,1)S(1)}, u32[]{:S(2)}, u32[]{:S(2)}) collective-permute-start(bf16[4,32,256]{2,1,0:T(8,128)(2,1)S(1)} %get-tuple-element.47), channel_id=1, source_target_pairs={{0,4},{1,5},{2,6},{3,7},{4,0},{5,1},{6,2},{7,3},{8,12},{9,13},{10,... | collective-permute-start | bytes 196616 | tf_op jit(solution)/shard_map/ppermute | solution.py:197
  18.3 10.1 %collective-permute-start.6 = (bf16[4,32,256]{2,1,0:T(8,128)(2,1)S(1)}, bf16[4,32,256]{2,1,0:T(8,128)(2,1)S(1)}, u32[]{:S(2)}, u32[]{:S(2)}) collective-permute-start(bf16[4,32,256]{2,1,0:T(8,128)(2,1)S(1)} %get-tuple-element.48), channel_id=1, source_target_pairs={{0,5},{1,4},{2,7},{3,6},{4,1},{5,0},{6,3},{7,2},{8,13},{9,12},{10,... | collective-permute-start | bytes 196616 | tf_op jit(solution)/shard_map/ppermute | solution.py:197
  20.7 4.0 %collective-permute-start = (s32[8,8]{1,0:T(8,128)S(1)}, s32[8,8]{1,0:T(8,128)S(1)}, u32[]{:S(2)}, u32[]{:S(2)}) collective-permute-start(s32[8,8]{1,0:T(8,128)S(1)} %bitcast.6), channel_id=1, source_target_pairs={{0,8},{1,9},{2,10},{3,11},{4,12},{5,13},{6,14},{7,15},{8,0},{9,1},... | collective-permute-start | bytes 776 | tf_op jit(solution)/shard_map/ppermute | solution.py:197
  24.7 9.0 %collective-permute-start.3 = (bf16[8,32,256]{2,1,0:T(8,128)(2,1)S(1)}, bf16[8,32,256]{2,1,0:T(8,128)(2,1)S(1)}, u32[]{:S(2)}, u32[]{:S(2)}) collective-permute-start(bf16[8,32,256]{2,1,0:T(8,128)(2,1)S(1)} %get-tuple-element.45), channel_id=1, source_target_pairs={{0,2},{1,3},{2,0},{3,1},{4,6},{5,7},{6,4},{7,5},{8,10},{9,11},{10,... | collective-permute-start | bytes 393224 | tf_op jit(solution)/shard_map/ppermute | solution.py:197
  24.9 8.8 %collective-permute-start.4 = (bf16[8,32,256]{2,1,0:T(8,128)(2,1)S(1)}, bf16[8,32,256]{2,1,0:T(8,128)(2,1)S(1)}, u32[]{:S(2)}, u32[]{:S(2)}) collective-permute-start(bf16[8,32,256]{2,1,0:T(8,128)(2,1)S(1)} %get-tuple-element.46), channel_id=1, source_target_pairs={{0,3},{1,2},{2,1},{3,0},{4,7},{5,6},{6,5},{7,4},{8,11},{9,10},{10,... | collective-permute-start | bytes 393224 | tf_op jit(solution)/shard_map/ppermute | solution.py:197
  27.6 6.4 %collective-permute-start.7 = (bf16[8,32,256]{2,1,0:T(8,128)(2,1)S(1)}, bf16[8,32,256]{2,1,0:T(8,128)(2,1)S(1)}, u32[]{:S(2)}, u32[]{:S(2)}) collective-permute-start(bf16[8,32,256]{2,1,0:T(8,128)(2,1)S(1)} %get-tuple-element.49), channel_id=1, source_target_pairs={{0,6},{1,7},{2,4},{3,5},{4,2},{5,3},{6,0},{7,1},{8,14},{9,15},{10,... | collective-permute-start | bytes 393224 | tf_op jit(solution)/shard_map/ppermute | solution.py:197
  28.5 7.6 %collective-permute-start.8 = (bf16[8,32,256]{2,1,0:T(8,128)(2,1)S(1)}, bf16[8,32,256]{2,1,0:T(8,128)(2,1)S(1)}, u32[]{:S(2)}, u32[]{:S(2)}) collective-permute-start(bf16[8,32,256]{2,1,0:T(8,128)(2,1)S(1)} %get-tuple-element.50), channel_id=1, source_target_pairs={{0,7},{1,6},{2,5},{3,4},{4,3},{5,2},{6,1},{7,0},{8,15},{9,14},{10,... | collective-permute-start | bytes 393224 | tf_op jit(solution)/shard_map/ppermute | solution.py:197
  29.4 6.6 %collective-permute-start.10 = (bf16[16,32,256]{2,1,0:T(8,128)(2,1)S(1)}, bf16[16,32,256]{2,1,0:T(8,128)(2,1)S(1)}, u32[]{:S(2)}, u32[]{:S(2)}) collective-permute-start(bf16[16,32,256]{2,1,0:T(8,128)(2,1)S(1)} %collective-permute-done.9.refs_8_), channel_id=1, source_target_pairs={{0,1},{1,0},{2,3},{3,2},{4,5},{5,4},{6,7},{7,6},{8,9},{9,8},{10,11... | collective-permute-start | bytes 786440 | tf_op jit(solution)/shard_map/ppermute | solution.py:197
